TPU v7x, 256 devices: a whole 4x4x8 slice. The times are simulated.
256 devices in a mesh: dp: 8 (over z_hi, x), ha: 4 (over y), wa: 8 (over z_lo, core).
Axes of the slice: x: 4, y: 4, z: 8 (z_hi: 2, z_lo: 4; z = z_hi * 4 + z_lo), core: 2. Of those that a mesh axis runs over, the one named last changes fastest.
Arguments:
- queries: bfloat16 [8, 1, 4, 8, 144, 768], P('dp', None, 'ha', 'wa'), may hold values from -5 to 5
- key_tiles: bfloat16 [8, 1, 4, 8, 144, 768], P('dp', None, 'ha', 'wa'), may hold values from -5 to 5
- value_tiles: bfloat16 [8, 1, 4, 8, 144, 768], P('dp', None, 'ha', 'wa'), may hold values from -6 to 6
- out_grad: bfloat16 [8, 1, 4, 8, 144, 1536], P('dp', None, 'ha', 'wa'), may hold values from -8 to 8
- w_out: bfloat16 [1536, 768], replicated, may hold values from -0.21875 to 0.21875
- reaches: int32 [6, 6], replicated, may hold values from 0 to 1, as said below
Outputs:
- grad_query: bfloat16 [8, 1, 4, 8, 144, 768], P('dp', None, 'ha', 'wa')
- grad_key: bfloat16 [8, 1, 4, 8, 144, 768], P('dp', None, 'ha', 'wa')
- grad_value: bfloat16 [8, 1, 4, 8, 144, 768], P('dp', None, 'ha', 'wa')
- grad_w_out: float32 [1536, 768], P(('dp', 'ha', 'wa'))
Inputs may be any that keep to these rules, and one draw needn't show every extreme that they name: `reaches`: some head has every entry 1, and some other head has every entry 0.
All inputs are finite; a program needn't handle non-finite values.
Results may differ from a plain program's by a relative error of at most 0.018.
Values may be sent and summed in bfloat16 or wider, within the bound.
A program may use at most 128 MiB of HBM per device.

v0:
```python
import math

import jax
import jax.numpy as jnp
from jax import lax
from jax.sharding import PartitionSpec as P

HEADS = 6
HD = 128


def shifted(block, axis, distance):
    devices = range(lax.axis_size(axis))
    route = [(i - distance, i) for i in devices if i - distance in devices]
    return lax.ppermute(block, axis, route)


def padded_2(array, sides, width):
    for axis, dim in sides:
        size, length = (lax.axis_size(axis), array.shape[dim])
        up = [(i, (i + 1) % size) for i in range(size - 1)]
        down = [(j, i) for i, j in up]
        last = lax.slice_in_dim(array, length - width, length, axis=dim)
        initial = lax.slice_in_dim(array, 0, width, axis=dim)
        before = lax.ppermute(last, axis, up)
        after = lax.ppermute(initial, axis, down)
        array = jnp.concatenate([before, array, after], axis=dim)
    return array


def split_up(array, dim, size):
    shape = array.shape
    parts = array.reshape(*shape[:dim], size, shape[dim] // size, *shape[dim + 1 :])
    return jnp.moveaxis(parts, dim, 0)


def sent_and_summed(array, axis, dim):
    size = lax.axis_size(axis)
    parts = lax.all_to_all(split_up(array, dim, size), axis, 0, 0, tiled=True)
    return jnp.sum(parts.astype(jnp.float32), axis=0)


def sum_at_owner(array, axis, dim):
    size = lax.axis_size(axis)
    parts = lax.all_to_all(split_up(array, dim, size), axis, 0, 0, tiled=True)
    return jnp.sum(parts, axis=0)


def tile_allowed(reach_row, t_count, row_base, col_base, row_total, col_total):
    time_ids = jnp.arange(t_count)
    t_delta = time_ids[None, :] - time_ids[:, None]
    time_ok = (t_delta >= -reach_row[0]) & (t_delta <= reach_row[1])
    offsets = jnp.arange(3) - 1
    row_ok = (
        (offsets >= -reach_row[2])
        & (offsets <= reach_row[3])
        & (row_base + offsets >= 0)
        & (row_base + offsets < row_total)
    )
    col_ok = (
        (offsets >= -reach_row[4])
        & (offsets <= reach_row[5])
        & (col_base + offsets >= 0)
        & (col_base + offsets < col_total)
    )
    return time_ok[:, :, None, None] & row_ok[None, None, :, None] & col_ok[None, None, None, :]


def pass_along_width(edge_piece, offset):
    return shifted(edge_piece.astype(jnp.bfloat16), "wa", offset).astype(edge_piece.dtype)


def pass_along_height(edge_piece, offset):
    return shifted(edge_piece.astype(jnp.bfloat16), "ha", offset).astype(edge_piece.dtype)


def shards(queries, key_tiles, value_tiles, out_grad, w_out, reaches):
    t_count = queries.shape[1]
    tile_len = queries.shape[4]
    width_q = queries.shape[5]
    model_width = out_grad.shape[5]
    token_rows = t_count * tile_len
    key_count = t_count * 9 * tile_len
    softmax_scale = 1.0 / math.sqrt(HD)
    row_base = lax.axis_index("ha")
    col_base = lax.axis_index("wa")
    row_total = lax.axis_size("ha")
    col_total = lax.axis_size("wa")
    key_value = jnp.concatenate([key_tiles, value_tiles], axis=5)
    padded = padded_2(key_value, (("ha", 2), ("wa", 3)), 1)
    padded = padded.reshape(key_count, 2 * width_q)
    query_rows = queries.reshape(token_rows, width_q)
    grad_rows = out_grad.reshape(token_rows, model_width)
    grad_attn = jnp.dot(grad_rows, w_out, preferred_element_type=jnp.float32).astype(jnp.bfloat16)
    attn_list, gq_list, gk_list, gv_list = ([], [], [], [])
    for head_index in range(HEADS):
        col_start = head_index * HD
        col_stop = col_start + HD
        query_head = query_rows[:, col_start:col_stop]
        key_head = padded[:, col_start:col_stop]
        value_head = padded[:, width_q + col_start : width_q + col_stop]
        grad_head = grad_attn[:, col_start:col_stop]
        tile_pairs = tile_allowed(
            reaches[head_index], t_count, row_base, col_base, row_total, col_total
        )
        allowed = jnp.broadcast_to(
            tile_pairs[:, None, :, :, :, None], (t_count, tile_len, t_count, 3, 3, tile_len)
        ).reshape(token_rows, key_count)
        scores = (
            jnp.einsum("ad,bd->ab", query_head, key_head, preferred_element_type=jnp.float32)
            * softmax_scale
        )
        masked = jnp.where(allowed, scores, -jnp.inf)
        row_peak = jnp.max(masked, axis=1, keepdims=True)
        exp_terms = jnp.exp(masked - row_peak)
        prob_rows = exp_terms / jnp.sum(exp_terms, axis=1, keepdims=True)
        probs_low = prob_rows.astype(jnp.bfloat16)
        attn_head = jnp.dot(probs_low, value_head, preferred_element_type=jnp.float32).astype(
            jnp.bfloat16
        )
        row_delta = jnp.sum(
            grad_head.astype(jnp.float32) * attn_head.astype(jnp.float32), axis=1, keepdims=True
        )
        grad_probs = jnp.einsum(
            "ad,bd->ab", grad_head, value_head, preferred_element_type=jnp.float32
        )
        grad_scores = (prob_rows * (grad_probs - row_delta)).astype(jnp.bfloat16)
        grad_q_head = (
            jnp.dot(grad_scores, key_head, preferred_element_type=jnp.float32) * softmax_scale
        ).astype(jnp.bfloat16)
        grad_k_head = (
            jnp.einsum("ab,ad->bd", grad_scores, query_head, preferred_element_type=jnp.float32)
            * softmax_scale
        )
        grad_v_head = jnp.einsum(
            "ab,ad->bd", probs_low, grad_head, preferred_element_type=jnp.float32
        )
        attn_list.append(attn_head)
        gq_list.append(grad_q_head)
        gk_list.append(grad_k_head)
        gv_list.append(grad_v_head)
    attended = jnp.concatenate(attn_list, axis=1)
    grad_query = jnp.concatenate(gq_list, axis=1).reshape(queries.shape)
    partial_value = jnp.concatenate(gk_list + gv_list, axis=1).reshape(
        t_count, 3, 3, tile_len, 2 * width_q
    )
    from_right = pass_along_width(partial_value[:, :, 0], -1)
    from_left = pass_along_width(partial_value[:, :, 2], 1)
    middle = partial_value[:, :, 1] + from_right + from_left
    summed = middle[:, 1] + pass_along_height(middle[:, 0], -1) + pass_along_height(middle[:, 2], 1)
    grad_key = summed[:, :, :width_q].astype(jnp.bfloat16).reshape(queries.shape)
    grad_value = summed[:, :, width_q:].astype(jnp.bfloat16).reshape(queries.shape)
    coarse = sent_and_summed(
        lax.dot_general(
            grad_rows, attended, (((0,), (0,)), ((), ())), preferred_element_type=jnp.float32
        ).astype(jnp.bfloat16),
        "dp",
        0,
    )
    grad_w_out = sum_at_owner(coarse, ("ha", "wa"), 0)
    return (grad_query, grad_key, grad_value, grad_w_out)


def solution(mesh):
    in_specs = (
        P("dp", None, "ha", "wa", None, None),
        P("dp", None, "ha", "wa", None, None),
        P("dp", None, "ha", "wa", None, None),
        P("dp", None, "ha", "wa", None, None),
        P(),
        P(),
    )
    out_specs = (
        P("dp", None, "ha", "wa", None, None),
        P("dp", None, "ha", "wa", None, None),
        P("dp", None, "ha", "wa", None, None),
        P(("dp", "ha", "wa"), None),
    )
    return jax.shard_map(shards, mesh=mesh, in_specs=in_specs, out_specs=out_specs, check_vma=False)
```

profile of v0, /device:TPU:1, one launch (start us, length us, event | category | flops | bytes accessed | tf_op | source)
XLA Modules:
  0.0 191.5 jit_solution(6622777393933172297)
XLA Ops:
  0.7 1.1 constant_dynamic-update-slice_fusion.1
  1.8 1.0 constant_dynamic-update-slice_fusion
  2.7 1.3 collective-permute-start.1
  4.0 5.4 %collective-permute-start = (bf16[1,1,1,1,144,1536]{5,4,3,2,1,0:T(8,128)(2,1)S(1)}, bf16[1,1,1,1,144,1536]{5,4,3,2,1,0:T(8,128)(2,1)}, u32[]{:S(2)}, u32[]{:S(2)}) collective-permute-start(bf16[1,1,1,1,144,1536]{5,4,3,2,1,0:T(8,128)(2,1)S(1)} %constant_dynamic-update-slice_fusion), channel_id=1, source_target_pairs={{0,8},{8,16},{16,24},{1,9},{9,17},{17,25},{2,10},{10,18},{18,26},{... | collective-permute-start | bytes 1327112 | tf_op jit(solution)/shard_map/ppermute | solution.py:25
  9.4 2.0 %fusion.125 = (s32[1,1]{1,0:T(1,128)}, s32[1,1]{1,0:T(1,128)}, s32[1,1]{1,0:T(1,128)}, s32[1,1]{1,0:T(1,128)}, s32[1,1]{1,0:T(1,128)}, /*index=5*/s32[1,1]{1,0:T...) fusion(s32[6,6]{1,0:T(8,128)} %param.11), kind=kLoop, calls=%fused_computation.207 | loop fusion | bytes 136 | tf_op jit(solution)/shard_map/slice | solution.py:55
  16.5 1.2 and_and_fusion.8
  17.7 1.3 and_and_fusion.9
  22.1 2.1 %fusion.124 = (s32[1,1]{1,0:T(1,128)}, s32[1,1]{1,0:T(1,128)}, s32[1,1]{1,0:T(1,128)}, s32[1,1]{1,0:T(1,128)}, s32[1,1]{1,0:T(1,128)}, /*index=5*/s32[1,1]{1,0:T...) fusion(s32[6,6]{1,0:T(8,128)} %param.11), kind=kLoop, calls=%fused_computation.206 | loop fusion | bytes 152 | tf_op jit(solution)/shard_map/slice | solution.py:55
  31.8 1.3 and_and_fusion
  33.1 1.3 and_and_fusion.1
  34.5 2.4 %pad_maximum_fusion.1 = bf16[1,1,3,1,144,1536]{5,4,3,2,1,0:T(8,128)(2,1)} fusion(bf16[1,1,1,1,144,1536]{5,4,3,2,1,0:T(8,128)(2,1)} %collective-permute-done.1, bf16[1,1,1,1,144,1536]{5,4,3,2,1,0:T(8,128)(2,1)S(1)} %constant_dynamic-update-slice_fusion, bf16[1,1,1,1,144,1536]{5,4,3,2,1,0:T(8,128)(2,1)} %collective-permute-done), kind=kLoop, calls=%fused_computation.57 | loop fusion | flops 1327104 | bytes 2654208 | tf_op jit(solution)/shard_map/concatenate | solution.py:27
  36.8 5.0 %collective-permute-start.3 = (bf16[1,1,3,1,144,1536]{5,4,3,2,1,0:T(8,128)(2,1)}, bf16[1,1,3,1,144,1536]{5,4,3,2,1,0:T(8,128)(2,1)}, u32[]{:S(2)}, u32[]{:S(2)}) collective-permute-start(bf16[1,1,3,1,144,1536]{5,4,3,2,1,0:T(8,128)(2,1)} %pad_maximum_fusion.1), channel_id=1, source_target_pairs={{1,0},{2,1},{3,2},{4,3},{5,4},{6,5},{7,6},{9,8},{10,9},{11,10},{12... | collective-permute-start | bytes 3981320 | tf_op jit(solution)/shard_map/ppermute | solution.py:26
  41.9 1.9 %collective-permute-start.2 = (bf16[1,1,3,1,144,1536]{5,4,3,2,1,0:T(8,128)(2,1)}, bf16[1,1,3,1,144,1536]{5,4,3,2,1,0:T(8,128)(2,1)}, u32[]{:S(2)}, u32[]{:S(2)}) collective-permute-start(bf16[1,1,3,1,144,1536]{5,4,3,2,1,0:T(8,128)(2,1)} %pad_maximum_fusion.1), channel_id=1, source_target_pairs={{0,1},{1,2},{2,3},{3,4},{4,5},{5,6},{6,7},{8,9},{9,10},{10,11},{11... | collective-permute-start | bytes 3981320 | tf_op jit(solution)/shard_map/ppermute | solution.py:25
  44.3 1.3 and_and_fusion.4
  45.6 1.2 and_and_fusion.5
  47.9 9.6 %collective-permute-done.3 = bf16[1,1,3,1,144,1536]{5,4,3,2,1,0:T(8,128)(2,1)} collective-permute-done((bf16[1,1,3,1,144,1536]{5,4,3,2,1,0:T(8,128)(2,1)}, bf16[1,1,3,1,144,1536]{5,4,3,2,1,0:T(8,128)(2,1)}, u32[]{:S(2)}, u32[]{:S(2)}) %collective-permute-start.3) | collective-permute-done | bytes 1327136 | tf_op jit(solution)/shard_map/ppermute | solution.py:26
  57.4 1.4 collective-permute-done.2
  58.8 2.2 %pad_maximum_fusion = bf16[1,1,3,3,144,1536]{5,4,3,2,1,0:T(8,128)(2,1)S(1)} fusion(bf16[1,1,3,1,144,1536]{5,4,3,2,1,0:T(8,128)(2,1)} %collective-permute-done.3, bf16[1,1,1,1,144,1536]{5,4,3,2,1,0:T(8,128)(2,1)} %collective-permute-done.1, bf16[1,1,1,1,144,1536]{5,4,3,2,1,0:T(8,128)(2,1)S(1)} %constant_dynamic-update-slice_fusion, ...), kind=kLoop, calls=%fused_computation.1 | loop fusion | flops 7962624 | bytes 7962624 | tf_op jit(solution)/shard_map/concatenate | solution.py:27
  67.7 1.1 fusion.25
  68.8 1.0 fusion.24
  69.9 1.1 fusion.23
  70.9 1.1 fusion.22
  72.0 1.1 fusion.21
  73.1 2.3 %fusion = bf16[1536,768]{0,1:T(8,128)(2,1)} fusion(bf16[144,768]{1,0:T(8,128)(2,1)S(1)} %constant_dynamic-update-slice_fusion.2, bf16[1,1,1,1,144,1536]{5,4,3,2,1,0:T(8,128)(2,1)S(1)} %copy-done.2), kind=kOutput, calls=%fused_computation.3 | convolution fusion | flops 340918272 | bytes 3022848 | tf_op jit(solution)/shard_map/dot_general | solution.py:154
  75.4 4.4 %copy.14 = bf16[1536,768]{1,0:T(8,128)(2,1)} copy(bf16[1536,768]{0,1:T(8,128)(2,1)} %fusion) | data formatting | bytes 4718592 | tf_op jit(solution)/shard_map/convert_element_type | solution.py:156
  79.7 9.7 %all-to-all-start = ((bf16[8,192,768]{2,1,0:T(8,128)(2,1)}), bf16[8,192,768]{2,1,0:T(8,128)(2,1)}, u32[]{:S(2)}, u32[]{:S(2)}) async-start(bf16[8,192,768]{2,1,0:T(8,128)(2,1)} %bitcast.125), calls=%async_computation | async-start | bytes 4718592 | tf_op jit(solution)/shard_map/all_to_all | solution.py:39
  89.5 1.5 fusion.20
  90.9 1.4 fusion.19
  92.3 1.5 fusion.18
  93.8 1.4 fusion.17
  99.8 1.9 %collective-permute-start.4 = (bf16[1,3,144,1536]{3,2,1,0:T(8,128)(2,1)S(1)}, bf16[1,3,144,1536]{3,2,1,0:T(8,128)(2,1)S(1)}, u32[]{:S(2)}, u32[]{:S(2)}) collective-permute-start(bf16[1,3,144,1536]{3,2,1,0:T(8,128)(2,1)S(1)} %get-tuple-element.12), channel_id=1, source_target_pairs={{1,0},{2,1},{3,2},{4,3},{5,4},{6,5},{7,6},{9,8},{10,9},{11,10},{12... | collective-permute-start | bytes 3981320 | tf_op jit(solution)/shard_map/ppermute | solution.py:15
  101.7 4.7 %collective-permute-start.5 = (bf16[1,3,144,1536]{3,2,1,0:T(8,128)(2,1)S(1)}, bf16[1,3,144,1536]{3,2,1,0:T(8,128)(2,1)S(1)}, u32[]{:S(2)}, u32[]{:S(2)}) collective-permute-start(bf16[1,3,144,1536]{3,2,1,0:T(8,128)(2,1)S(1)} %get-tuple-element.13), channel_id=1, source_target_pairs={{0,1},{1,2},{2,3},{3,4},{4,5},{5,6},{6,7},{8,9},{9,10},{10,11},{11... | collective-permute-start | bytes 3981320 | tf_op jit(solution)/shard_map/ppermute | solution.py:15
  106.4 1.2 fusion.28
  107.7 1.3 fusion.30
  109.0 1.3 fusion.32
  110.2 1.3 fusion.34
  111.5 35.0 %collective-permute-done.4 = bf16[1,3,144,1536]{3,2,1,0:T(8,128)(2,1)S(1)} collective-permute-done((bf16[1,3,144,1536]{3,2,1,0:T(8,128)(2,1)S(1)}, bf16[1,3,144,1536]{3,2,1,0:T(8,128)(2,1)S(1)}, u32[]{:S(2)}, u32[]{:S(2)}) %collective-permute-start.4) | collective-permute-done | bytes 1327136 | tf_op jit(solution)/shard_map/ppermute | solution.py:15
  146.5 2.2 %fusion.122 = (bf16[1,3,144,1536]{3,2,1,0:T(8,128)(2,1)S(1)}, f32[1,3,144,1536]{3,2,1,0:T(8,128)}) fusion(bf16[1,3,144,1536]{3,2,1,0:T(8,128)(2,1)S(1)} %collective-permute-done.5, bf16[1,3,144,1536]{3,2,1,0:T(8,128)(2,1)S(1)} %collective-permute-done.4, f32[1,3,3,144,1536]{4,3,2,1,0:T(8,128)S(1)} %bitcast.127), kind=kLoop, calls=%fused_computation.205 | loop fusion | flops 3317760 | bytes 9289728 | tf_op jit(solution)/shard_map/convert.3
  148.7 1.0 slice_bitcast_fusion.5
  149.7 1.3 collective-permute-start.6
  150.9 4.8 %collective-permute-start.7 = (bf16[1,144,1536]{2,1,0:T(8,128)(2,1)}, bf16[1,144,1536]{2,1,0:T(8,128)(2,1)}, u32[]{:S(2)}, u32[]{:S(2)}) collective-permute-start(bf16[1,144,1536]{2,1,0:T(8,128)(2,1)} %get-tuple-element.15), channel_id=1, source_target_pairs={{0,8},{8,16},{16,24},{1,9},{9,17},{17,25},{2,10},{10,18},{18,26},{... | collective-permute-start | bytes 1327112 | tf_op jit(solution)/shard_map/ppermute | solution.py:15
  155.7 2.0 %convert_reduce_fusion = f32[192,768]{1,0:T(8,128)S(1)} fusion(bf16[8,192,768]{2,1,0:T(8,128)(2,1)} %all-to-all-done), kind=kLoop, calls=%fused_computation | loop fusion | flops 2211840 | bytes 2949120 | tf_op jit(solution)/shard_map/reduce_sum | solution.py:40
  157.8 1.0 reshape.621
  158.8 9.7 %all-to-all-start.1 = ((f32[32,6,768]{2,1,0:T(8,128)}), f32[32,6,768]{2,1,0:T(8,128)S(1)}, u32[]{:S(2)}, u32[]{:S(2)}) async-start(f32[32,6,768]{2,1,0:T(8,128)} %reshape.621), calls=%async_computation.1 | async-start | bytes 1572864 | tf_op jit(solution)/shard_map/all_to_all | solution.py:45
  168.5 2.0 %fusion.36 = bf16[144,768]{1,0:T(8,128)(2,1)} fusion(bf16[144,768]{1,0:T(8,128)(2,1)} %copy-done.25, bf16[144,1296]{1,0:T(8,128)(2,1)} %fusion.25, bf16[1296,1536]{1,0:T(8,128)(2,1)} %bitcast.150), kind=kOutput, calls=%fused_computation.74 | convolution fusion | flops 47812608 | bytes 774144 | tf_op jit(solution)/shard_map/dot_general | solution.py:129
  170.5 1.9 fusion.38
  172.4 1.6 fusion.41
  174.7 16.1 %all-to-all-done.1 = f32[32,6,768]{2,1,0:T(8,128)S(1)} async-done(((f32[32,6,768]{2,1,0:T(8,128)}), f32[32,6,768]{2,1,0:T(8,128)S(1)}, u32[]{:S(2)}, u32[]{:S(2)}) %all-to-all-start.1) | async-done | bytes 589856 | tf_op jit(solution)/shard_map/all_to_all | solution.py:45
  (108 shorter events, 14.6 us)
Async XLA Ops:
  0.6 46.7 %copy-start = (bf16[1536,768]{1,0:T(8,128)(2,1)S(1)}, bf16[1536,768]{1,0:T(8,128)(2,1)}, u32[]{:S(2)}) copy-start(bf16[1536,768]{1,0:T(8,128)(2,1)} %param.10) | copy-start | bytes 7077892
  0.6 46.7 %copy-start.2 = (bf16[1,1,1,1,144,1536]{5,4,3,2,1,0:T(8,128)(2,1)S(1)}, bf16[1,1,1,1,144,1536]{5,4,3,2,1,0:T(8,128)(2,1)}, u32[]{:S(2)}) copy-start(bf16[1,1,1,1,144,1536]{5,4,3,2,1,0:T(8,128)(2,1)} %param.9) | copy-start | bytes 1327108
  2.7 31.7 %collective-permute-start.1 = (bf16[1,1,1,1,144,1536]{5,4,3,2,1,0:T(8,128)(2,1)S(1)}, bf16[1,1,1,1,144,1536]{5,4,3,2,1,0:T(8,128)(2,1)}, u32[]{:S(2)}, u32[]{:S(2)}) collective-permute-start(bf16[1,1,1,1,144,1536]{5,4,3,2,1,0:T(8,128)(2,1)S(1)} %constant_dynamic-update-slice_fusion), channel_id=1, source_target_pairs={{8,0},{16,8},{24,16},{9,1},{17,9},{25,17},{10,2},{18,10},{26,18},{... | collective-permute-start | bytes 1327112 | tf_op jit(solution)/shard_map/ppermute | solution.py:26
  4.0 30.4 %collective-permute-start = (bf16[1,1,1,1,144,1536]{5,4,3,2,1,0:T(8,128)(2,1)S(1)}, bf16[1,1,1,1,144,1536]{5,4,3,2,1,0:T(8,128)(2,1)}, u32[]{:S(2)}, u32[]{:S(2)}) collective-permute-start(bf16[1,1,1,1,144,1536]{5,4,3,2,1,0:T(8,128)(2,1)S(1)} %constant_dynamic-update-slice_fusion), channel_id=1, source_target_pairs={{0,8},{8,16},{16,24},{1,9},{9,17},{17,25},{2,10},{10,18},{18,26},{... | collective-permute-start | bytes 1327112 | tf_op jit(solution)/shard_map/ppermute | solution.py:25
  36.8 20.6 %collective-permute-start.3 = (bf16[1,1,3,1,144,1536]{5,4,3,2,1,0:T(8,128)(2,1)}, bf16[1,1,3,1,144,1536]{5,4,3,2,1,0:T(8,128)(2,1)}, u32[]{:S(2)}, u32[]{:S(2)}) collective-permute-start(bf16[1,1,3,1,144,1536]{5,4,3,2,1,0:T(8,128)(2,1)} %pad_maximum_fusion.1), channel_id=1, source_target_pairs={{1,0},{2,1},{3,2},{4,3},{5,4},{6,5},{7,6},{9,8},{10,9},{11,10},{12... | collective-permute-start | bytes 3981320 | tf_op jit(solution)/shard_map/ppermute | solution.py:26
  41.9 17.0 %collective-permute-start.2 = (bf16[1,1,3,1,144,1536]{5,4,3,2,1,0:T(8,128)(2,1)}, bf16[1,1,3,1,144,1536]{5,4,3,2,1,0:T(8,128)(2,1)}, u32[]{:S(2)}, u32[]{:S(2)}) collective-permute-start(bf16[1,1,3,1,144,1536]{5,4,3,2,1,0:T(8,128)(2,1)} %pad_maximum_fusion.1), channel_id=1, source_target_pairs={{0,1},{1,2},{2,3},{3,4},{4,5},{5,6},{6,7},{8,9},{9,10},{10,11},{11... | collective-permute-start | bytes 3981320 | tf_op jit(solution)/shard_map/ppermute | solution.py:25
  47.8 24.1 %copy-start.23 = (bf16[144,768]{1,0:T(8,128)(2,1)}, bf16[144,768]{1,0:T(8,128)(2,1)S(1)}, u32[]{:S(2)}) copy-start(bf16[144,768]{1,0:T(8,128)(2,1)S(1)} %convolution_convert_fusion.1) | copy-start | bytes 663556
  47.9 13.2 %copy-start.22 = (bf16[1,1,1,1,144,768]{5,4,3,2,1,0:T(8,128)(2,1)S(1)}, bf16[1,1,1,1,144,768]{5,4,3,2,1,0:T(8,128)(2,1)}, u32[]{:S(2)}) copy-start(bf16[1,1,1,1,144,768]{5,4,3,2,1,0:T(8,128)(2,1)} %param.6) | copy-start | bytes 663556
  61.0 11.0 %copy-start.1 = (bf16[1,1,3,3,144,1536]{5,4,3,2,1,0:T(8,128)(2,1)}, bf16[1,1,3,3,144,1536]{5,4,3,2,1,0:T(8,128)(2,1)S(1)}, u32[]{:S(2)}) copy-start(bf16[1,1,3,3,144,1536]{5,4,3,2,1,0:T(8,128)(2,1)S(1)} %pad_maximum_fusion) | copy-start | bytes 11943940
  61.4 6.0 %copy-start.3 = (f32[1296,144]{0,1:T(8,128)}, f32[1296,144]{0,1:T(8,128)S(1)}, u32[]{:S(2)}) copy-start(f32[1296,144]{0,1:T(8,128)S(1)} %get-tuple-element.55) | copy-start | bytes 2239492
  61.8 5.9 %copy-start.5 = (f32[1296,144]{0,1:T(8,128)}, f32[1296,144]{0,1:T(8,128)S(1)}, u32[]{:S(2)}) copy-start(f32[1296,144]{0,1:T(8,128)S(1)} %get-tuple-element.65) | copy-start | bytes 2239492
  62.2 6.6 %copy-start.7 = (f32[1296,144]{0,1:T(8,128)}, f32[1296,144]{0,1:T(8,128)S(1)}, u32[]{:S(2)}) copy-start(f32[1296,144]{0,1:T(8,128)S(1)} %get-tuple-element.63) | copy-start | bytes 2239492
  62.6 7.2 %copy-start.9 = (f32[1296,144]{0,1:T(8,128)}, f32[1296,144]{0,1:T(8,128)S(1)}, u32[]{:S(2)}) copy-start(f32[1296,144]{0,1:T(8,128)S(1)} %get-tuple-element.61) | copy-start | bytes 2239492
  63.0 7.9 %copy-start.11 = (f32[1296,144]{0,1:T(8,128)}, f32[1296,144]{0,1:T(8,128)S(1)}, u32[]{:S(2)}) copy-start(f32[1296,144]{0,1:T(8,128)S(1)} %get-tuple-element.59) | copy-start | bytes 2239492
  63.4 8.6 %copy-start.13 = (f32[1296,144]{0,1:T(8,128)}, f32[1296,144]{0,1:T(8,128)S(1)}, u32[]{:S(2)}) copy-start(f32[1296,144]{0,1:T(8,128)S(1)} %get-tuple-element.57) | copy-start | bytes 2239492
  67.7 27.9 %copy-start.15 = (bf16[144,1296]{1,0:T(8,128)(2,1)}, bf16[144,1296]{1,0:T(8,128)(2,1)S(1)}, u32[]{:S(2)}) copy-start(bf16[144,1296]{1,0:T(8,128)(2,1)S(1)} %fusion.26) | copy-start | bytes 1119748
  79.7 15.5 %copy-start.17 = (bf16[144,1296]{1,0:T(8,128)(2,1)S(1)}, bf16[144,1296]{1,0:T(8,128)(2,1)}, u32[]{:S(2)}) copy-start(bf16[144,1296]{1,0:T(8,128)(2,1)} %fusion.25) | copy-start | bytes 1119748
  79.7 76.0 %all-to-all-start = ((bf16[8,192,768]{2,1,0:T(8,128)(2,1)}), bf16[8,192,768]{2,1,0:T(8,128)(2,1)}, u32[]{:S(2)}, u32[]{:S(2)}) async-start(bf16[8,192,768]{2,1,0:T(8,128)(2,1)} %bitcast.125), calls=%async_computation | async-start | bytes 4718592 | tf_op jit(solution)/shard_map/all_to_all | solution.py:39
  89.4 6.6 %copy-start.14 = (f32[1296,144]{0,1:T(8,128)S(1)}, f32[1296,144]{0,1:T(8,128)}, u32[]{:S(2)}) copy-start(f32[1296,144]{0,1:T(8,128)} %copy-done.13) | copy-start | bytes 2239492
  89.4 6.6 %copy-start.24 = (bf16[144,768]{1,0:T(8,128)(2,1)S(1)}, bf16[144,768]{1,0:T(8,128)(2,1)}, u32[]{:S(2)}) copy-start(bf16[144,768]{1,0:T(8,128)(2,1)} %copy-done.23) | copy-start | bytes 663556
  92.3 4.2 %copy-start.12 = (f32[1296,144]{0,1:T(8,128)S(1)}, f32[1296,144]{0,1:T(8,128)}, u32[]{:S(2)}) copy-start(f32[1296,144]{0,1:T(8,128)} %copy-done.11) | copy-start | bytes 2239492
  95.6 1.4 copy-start.10
  96.5 1.2 copy-start.8
  97.1 1.2 copy-start.6
  97.7 1.2 copy-start.4
  98.9 7.5 %copy-start.21 = (bf16[144,1296]{1,0:T(8,128)(2,1)S(1)}, bf16[144,1296]{1,0:T(8,128)(2,1)}, u32[]{:S(2)}) copy-start(bf16[144,1296]{1,0:T(8,128)(2,1)} %fusion.21) | copy-start | bytes 1119748
  98.9 8.7 %copy-start.20 = (bf16[144,1296]{1,0:T(8,128)(2,1)S(1)}, bf16[144,1296]{1,0:T(8,128)(2,1)}, u32[]{:S(2)}) copy-start(bf16[144,1296]{1,0:T(8,128)(2,1)} %fusion.22) | copy-start | bytes 1119748
  99.4 9.5 %copy-start.19 = (bf16[144,1296]{1,0:T(8,128)(2,1)S(1)}, bf16[144,1296]{1,0:T(8,128)(2,1)}, u32[]{:S(2)}) copy-start(bf16[144,1296]{1,0:T(8,128)(2,1)} %fusion.23) | copy-start | bytes 1119748
  99.4 10.8 %copy-start.18 = (bf16[144,1296]{1,0:T(8,128)(2,1)S(1)}, bf16[144,1296]{1,0:T(8,128)(2,1)}, u32[]{:S(2)}) copy-start(bf16[144,1296]{1,0:T(8,128)(2,1)} %fusion.24) | copy-start | bytes 1119748
  99.8 46.7 %collective-permute-start.4 = (bf16[1,3,144,1536]{3,2,1,0:T(8,128)(2,1)S(1)}, bf16[1,3,144,1536]{3,2,1,0:T(8,128)(2,1)S(1)}, u32[]{:S(2)}, u32[]{:S(2)}) collective-permute-start(bf16[1,3,144,1536]{3,2,1,0:T(8,128)(2,1)S(1)} %get-tuple-element.12), channel_id=1, source_target_pairs={{1,0},{2,1},{3,2},{4,3},{5,4},{6,5},{7,6},{9,8},{10,9},{11,10},{12... | collective-permute-start | bytes 3981320 | tf_op jit(solution)/shard_map/ppermute | solution.py:15
  101.7 44.7 %collective-permute-start.5 = (bf16[1,3,144,1536]{3,2,1,0:T(8,128)(2,1)S(1)}, bf16[1,3,144,1536]{3,2,1,0:T(8,128)(2,1)S(1)}, u32[]{:S(2)}, u32[]{:S(2)}) collective-permute-start(bf16[1,3,144,1536]{3,2,1,0:T(8,128)(2,1)S(1)} %get-tuple-element.13), channel_id=1, source_target_pairs={{0,1},{1,2},{2,3},{3,4},{4,5},{5,6},{6,7},{8,9},{9,10},{10,11},{11... | collective-permute-start | bytes 3981320 | tf_op jit(solution)/shard_map/ppermute | solution.py:15
  111.5 35.0 %copy-start.25 = (bf16[144,768]{1,0:T(8,128)(2,1)}, bf16[144,768]{1,0:T(8,128)(2,1)S(1)}, u32[]{:S(2)}) copy-start(bf16[144,768]{1,0:T(8,128)(2,1)S(1)} %fusion.34) | copy-start | bytes 663556
  148.7 21.8 %copy-start.16 = (bf16[144,1296]{1,0:T(8,128)(2,1)S(1)}, bf16[144,1296]{1,0:T(8,128)(2,1)}, u32[]{:S(2)}) copy-start(bf16[144,1296]{1,0:T(8,128)(2,1)} %copy-done.15) | copy-start | bytes 1119748
  149.7 22.7 %collective-permute-start.6 = (bf16[1,144,1536]{2,1,0:T(8,128)(2,1)}, bf16[1,144,1536]{2,1,0:T(8,128)(2,1)}, u32[]{:S(2)}, u32[]{:S(2)}) collective-permute-start(bf16[1,144,1536]{2,1,0:T(8,128)(2,1)} %get-tuple-element.14), channel_id=1, source_target_pairs={{8,0},{16,8},{24,16},{9,1},{17,9},{25,17},{10,2},{18,10},{26,18},{... | collective-permute-start | bytes 1327112 | tf_op jit(solution)/shard_map/ppermute | solution.py:15
  150.9 21.4 %collective-permute-start.7 = (bf16[1,144,1536]{2,1,0:T(8,128)(2,1)}, bf16[1,144,1536]{2,1,0:T(8,128)(2,1)}, u32[]{:S(2)}, u32[]{:S(2)}) collective-permute-start(bf16[1,144,1536]{2,1,0:T(8,128)(2,1)} %get-tuple-element.15), channel_id=1, source_target_pairs={{0,8},{8,16},{16,24},{1,9},{9,17},{17,25},{2,10},{10,18},{18,26},{... | collective-permute-start | bytes 1327112 | tf_op jit(solution)/shard_map/ppermute | solution.py:15
  158.8 32.1 %all-to-all-start.1 = ((f32[32,6,768]{2,1,0:T(8,128)}), f32[32,6,768]{2,1,0:T(8,128)S(1)}, u32[]{:S(2)}, u32[]{:S(2)}) async-start(f32[32,6,768]{2,1,0:T(8,128)} %reshape.621), calls=%async_computation.1 | async-start | bytes 1572864 | tf_op jit(solution)/shard_map/all_to_all | solution.py:45
where the time goes:
time: 193 us; the launch traced here: 191 us
  waiting for transfers between devices  62 us (32%)
  starting transfers between devices  45.7 us (24%)
  matrix products  31.4 us (16%)
  other arithmetic  20.7 us (11%)
  between operations  16.4 us (8%)
  local copies, waits for them, and re-layouts  15.2 us (8%)
    ppermute x4, waiting for transfers between devices, shifted(): return lax.ppermute(block, axis, route)  35 us
    all_to_all x1, waiting for transfers between devices, sum_at_owner(): parts = lax.all_to_all(split_up(array, dim, size), axis, 0, 0, tiled=True)  16.1 us
    ppermute x4, starting transfers between devices, shifted(): return lax.ppermute(block, axis, route)  12.7 us
    all_to_all x1, starting transfers between devices, sum_at_owner(): parts = lax.all_to_all(split_up(array, dim, size), axis, 0, 0, tiled=True)  9.75 us
    all_to_all x1, starting transfers between devices, sent_and_summed(): parts = lax.all_to_all(split_up(array, dim, size), axis, 0, 0, tiled=True)  9.69 us
    ppermute x2, waiting for transfers between devices, padded_2(): after = lax.ppermute(initial, axis, down)  9.57 us
    dot_general x6, matrix products, shards(): jnp.dot(grad_scores, key_head, preferred_element_type=jnp.float32)  8.88 us
    ppermute x2, starting transfers between devices, padded_2(): before = lax.ppermute(last, axis, up)  7.35 us
  transfers between devices with their start and end apart: 10, of which 4 were waited for; matrix products, arithmetic and copies ran while one was open for 21% of the time, Pallas kernels for 0%

commit v1 on v0

v1 whole, which is shorter than its diff:
```python
import math

import jax
import jax.numpy as jnp
from jax import lax
from jax.experimental import pallas as pl
from jax.experimental.pallas import tpu as pltpu
from jax.sharding import PartitionSpec as P

MESH = pl.DeviceIdType.MESH
HEADS = 6
HALO = 5
HD = 128
TILE = 144
KEYS = 9 * TILE
HQ = HEADS * HD
D = 1536
SCALE = 1.0 / math.sqrt(HD)
ROWS = 16
BF = jnp.bfloat16
F32 = jnp.float32
ANY_COLS = (0, 2)


def dot(a, b):
    return jnp.dot(a, b, preferred_element_type=F32)


def dot_nt(a, b):
    return lax.dot_general(a, b, (((1,), (1,)), ((), ())), preferred_element_type=F32)


def kernel(
    reach, q_in, k_in, v_in, og_in, w_in,
    gq_out, gk_out, gv_out, gw_out,
    q_v, k_v, v_v, og_v, w_v, a_v, ogt, kv, qa, kv0, qa0, stat, sb, trow,
    s_buf, dp_buf, p_buf, ds_buf, att_buf, res,
    gbuf, rbuf, abuf, x1buf, xs, x2buf, cbuf, ybuf, zbuf, zr, fbuf, f2, gws,
    in_sem, yk_s, yk_r, yq_s, yq_r, wk_s, wk_r, wq_s, wq_r, sy_s, sy_r, sw_s, sw_r,
    dd_s, dd_r, x1_s, x1_r, x2_s, x2_r, yy_s, yy_r, zz_s, zz_r, fin_s, fin_r,
):
    dp = lax.axis_index("dp")
    ha = lax.axis_index("ha")
    wa = lax.axis_index("wa")
    x = lax.rem(dp, 4)
    z_hi = lax.div(dp, 4)
    core = lax.rem(wa, 2)
    z_lo = lax.div(wa, 2)
    zi = z_hi * 4 + z_lo
    mate = wa + 1 - 2 * core
    x_one = x + 1 - 2 * lax.rem(x, 2)
    x_three = 3 - x
    x_far = lax.rem(x + 2, 4)
    x_a = x_one + core * (x_three - x_one)
    x_b = x_three + core * (x_one - x_three)
    has_left = wa > 0
    has_right = wa < 7

    def at(dp_=dp, ha_=ha, wa_=wa):
        return (dp_, ha_, wa_)

    barrier = pltpu.get_barrier_semaphore()

    def greet(device):
        pl.semaphore_signal(barrier, inc=1, device_id=device, device_id_type=MESH)

    for dy in (1, 2, 3):
        greet(at(ha_=lax.rem(ha + dy, 4)))
    greet(at(wa_=mate))
    greet(at(dp_=z_hi * 4 + x_one))
    greet(at(dp_=z_hi * 4 + x_three))

    def z_device(dz):
        zt = lax.rem(zi + dz, 8)
        return at(dp_=lax.div(zt, 4) * 4 + x, wa_=lax.rem(zt, 4) * 2 + core)

    for dz in range(1, 8):
        greet(z_device(dz))
    far_right = (core == 1) & has_right
    far_left = (core == 0) & has_left

    @pl.when(far_right)
    def _():
        greet(at(wa_=wa + 1))

    @pl.when(far_left)
    def _():
        greet(at(wa_=wa - 1))

    loads = [
        pltpu.make_async_copy(src, dst, in_sem.at[n])
        for n, (src, dst) in enumerate(
            ((k_in, k_v), (v_in, v_v), (q_in, q_v), (og_in, og_v), (w_in, w_v))
        )
    ]
    for load in loads:
        load.start()

    zero_head = jnp.int32(0)
    for n in reversed(range(HEADS)):
        total = reach[n, 0]
        for t in range(1, 6):
            total = total + reach[n, t]
        zero_head = jnp.where(total == 0, n, zero_head)

    def columns(ref, head):
        return ref[:, head * HD : (head + 1) * HD]

    def slot_columns(ref, slot):
        return jnp.where(slot >= zero_head, columns(ref, slot + 1), columns(ref, slot))

    def zero_columns(ref):
        value = columns(ref, 0)
        for h in range(1, HEADS):
            value = jnp.where(zero_head == h, columns(ref, h), value)
        return value

    def head_value(of_slot, h):
        value = jnp.where(zero_head == h, of_slot(HALO), of_slot(min(h, HALO - 1)))
        return jnp.where(zero_head < h, of_slot(h - 1), value) if h else value

    @pl.when(wa == 0)
    def _():
        for buf in (kv, qa):
            def clear(s, carry, buf=buf):
                for kind in range(2):
                    for r in range(3):
                        buf[s, kind, r, 0] = jnp.zeros((TILE, HD), BF)
                return carry
            lax.fori_loop(0, HALO, clear, 0)
        for r in range(3):
            sb[r, 0] = jnp.zeros((TILE, HD), BF)

    @pl.when(wa == 7)
    def _():
        for buf in (kv, qa):
            def clear(s, carry, buf=buf):
                for kind in range(2):
                    for r in range(3):
                        buf[s, kind, r, 2] = jnp.zeros((TILE, HD), BF)
                return carry
            lax.fori_loop(0, HALO, clear, 0)
        for r in range(3):
            sb[r, 2] = jnp.zeros((TILE, HD), BF)

    loads[0].wait()
    loads[1].wait()

    for s in range(HALO):
        kv[s, 0, 1, 1] = slot_columns(k_v, s)
        kv[s, 1, 1, 1] = slot_columns(v_v, s)
    kv0[0] = zero_columns(k_v)
    kv0[1] = zero_columns(v_v)

    ha_up = lax.rem(ha + 3, 4)
    ha_down = lax.rem(ha + 1, 4)
    wa_right = jnp.minimum(wa + 1, 7)
    wa_left = jnp.maximum(wa - 1, 0)

    def y_copy(buf, send, recv, s, r):
        return pltpu.make_async_remote_copy(
            src_ref=buf.at[s, :, 1, 1], dst_ref=buf.at[s, :, r, 1],
            send_sem=send.at[s, r // 2], recv_sem=recv.at[s, r // 2],
            device_id=at(ha_=ha_up if r == 2 else ha_down), device_id_type=MESH,
        )

    def w_copy(buf, send, recv, s, r, c):
        return pltpu.make_async_remote_copy(
            src_ref=buf.at[s, :, r, 1], dst_ref=buf.at[s, :, r, c],
            send_sem=send.at[s, r, c // 2], recv_sem=recv.at[s, r, c // 2],
            device_id=at(wa_=wa_right if c == 0 else wa_left), device_id_type=MESH,
        )

    sends_to = {0: has_right, 2: has_left}
    gets_from = {0: has_left, 2: has_right}

    def w_send(buf, send, recv, s, r):
        for c in ANY_COLS:
            @pl.when(sends_to[c])
            def _(c=c):
                w_copy(buf, send, recv, s, r, c).start()

    def relay(buf, y_send, y_recv, w_s, w_r, s):
        for r in (0, 2):
            y_copy(buf, y_send, y_recv, s, r).wait_recv()
            w_send(buf, w_s, w_r, s, r)

    def w_wait(buf, send, recv, s):
        for c in ANY_COLS:
            @pl.when(gets_from[c])
            def _(c=c):
                for r in range(3):
                    w_copy(buf, send, recv, s, r, c).wait_recv()

    def relay_kv(s):
        relay(kv, yk_s, yk_r, wk_s, wk_r, s)

    def relay_qa(s):
        relay(qa, yq_s, yq_r, wq_s, wq_r, s)

    pl.semaphore_wait(barrier, 13 + (far_right | far_left).astype(jnp.int32))

    def first_kv(s, carry):
        for r in (0, 2):
            y_copy(kv, yk_s, yk_r, s, r).start()
        w_send(kv, wk_s, wk_r, s, 1)
        return carry

    lax.fori_loop(0, HALO, first_kv, 0)

    loads[2].wait()
    loads[3].wait()
    loads[4].wait()
    a_v[...] = dot(og_v[...], w_v[...]).astype(BF)

    for s in range(HALO):
        qa[s, 0, 1, 1] = slot_columns(q_v, s)
        qa[s, 1, 1, 1] = slot_columns(a_v, s)
        for r in (0, 2):
            y_copy(qa, yq_s, yq_r, s, r).start()
    qa0[0] = zero_columns(q_v)
    qa0[1] = zero_columns(a_v)

    eye = (
        lax.broadcasted_iota(jnp.int32, (HD, HD), 0) == lax.broadcasted_iota(jnp.int32, (HD, HD), 1)
    ).astype(F32).astype(BF)
    for t in range(D // HD):
        ogt[t * HD : (t + 1) * HD, :] = dot_nt(eye, og_v[:, t * HD : (t + 1) * HD]).astype(BF)

    stat[...] = jnp.zeros((TILE, HD), F32)
    lane = lax.broadcasted_iota(jnp.int32, (ROWS, HD), 1)
    key_id = lax.broadcasted_iota(jnp.int32, (1, KEYS), 1)
    place = jnp.zeros((1, KEYS), jnp.int32)
    for n in range(1, 9):
        place = place + (key_id >= n * TILE).astype(jnp.int32)
    row_id = (key_id >= 3 * TILE).astype(jnp.int32) + (key_id >= 6 * TILE).astype(jnp.int32)
    col_id = place - 3 * row_id

    def bias_row(s, mirrored):
        later = s >= zero_head
        up, down, left, right = (jnp.where(later, reach[s + 1, t], reach[s, t]) for t in range(2, 6))
        if mirrored:
            up, down, left, right = down, up, right, left

        def bias(ok):
            return jnp.where(ok, 0.0, -jnp.inf).astype(F32)

        b_up = bias((up > 0) & (ha > 0))
        b_down = bias((down > 0) & (ha < 3))
        b_left = bias((left > 0) & has_left)
        b_right = bias((right > 0) & has_right)
        zero = jnp.zeros((1, KEYS), F32)
        by_row = jnp.where(row_id == 0, zero + b_up, jnp.where(row_id == 2, zero + b_down, zero))
        by_col = jnp.where(col_id == 0, zero + b_left, jnp.where(col_id == 2, zero + b_right, zero))
        return by_row + by_col

    def split3(value):
        high = value.astype(BF).astype(F32)
        rest = value - high
        mid = rest.astype(BF).astype(F32)
        return high, mid, rest - mid

    def forward(slot, q, a, k, v, bias):
        n = k.shape[0]
        s_buf[:, :n] = dot_nt(q, k)
        dp_buf[:, :n] = dot_nt(a, v)

        def rows_step(i, carry):
            rows = pl.ds(pl.multiple_of(i * ROWS, ROWS), ROWS)
            s = s_buf[rows, :n] * SCALE
            if bias is not None:
                s = s + bias
            d = dp_buf[rows, :n]
            peak = jnp.max(s, axis=1, keepdims=True)
            e = jnp.exp(s - peak)
            total = jnp.sum(e, axis=1, keepdims=True)
            p = e * (1.0 / total)
            delta = jnp.sum(p * d, axis=1, keepdims=True)
            p_buf[rows, :n] = p.astype(BF)
            ds_buf[rows, :n] = (p * (d - delta)).astype(BF)
            block = stat[rows, :]
            for base, parts in ((0, split3(peak + jnp.log(total))), (64, split3(delta))):
                for t, part in enumerate(parts):
                    block = jnp.where(lane == base + 3 * slot + t, part, block)
            stat[rows, :] = block
            return carry

        lax.fori_loop(0, TILE // ROWS, rows_step, 0)
        att_buf[...] = dot(p_buf[:, :n], v).astype(BF)
        res[0, slot] = (dot(ds_buf[:, :n], k) * SCALE).astype(BF)

    def backward(slot, k, v, q, a, lse_row, delta_row):
        n = q.shape[0]
        s_buf[:, :n] = dot_nt(k, q)
        dp_buf[:, :n] = dot_nt(v, a)

        def rows_step(i, carry):
            rows = pl.ds(pl.multiple_of(i * ROWS, ROWS), ROWS)
            p = jnp.exp(s_buf[rows, :n] * SCALE - lse_row)
            p_buf[rows, :n] = p.astype(BF)
            ds_buf[rows, :n] = (p * (dp_buf[rows, :n] - delta_row)).astype(BF)
            return carry

        lax.fori_loop(0, TILE // ROWS, rows_step, 0)
        res[2, slot] = dot(p_buf[:, :n], a).astype(BF)
        res[1, slot] = (dot(ds_buf[:, :n], q) * SCALE).astype(BF)

    def weight_term(index):
        def step(t, carry):
            rows = pl.ds(pl.multiple_of(t * 192, 192), 192)
            gbuf[index, lax.div(t, 4), lax.rem(t, 4)] = dot(ogt[rows, :], att_buf[...]).astype(BF)
            return carry

        lax.fori_loop(0, 8, step, 0)

    def mate_copy(j):
        return pltpu.make_async_remote_copy(
            src_ref=gbuf.at[2 * j + 1 - core], dst_ref=rbuf.at[j],
            send_sem=dd_s.at[j], recv_sem=dd_r.at[j], device_id=at(wa_=mate), device_id_type=MESH,
        )

    def x1_copy(j, which):
        return pltpu.make_async_remote_copy(
            src_ref=abuf.at[j, :, x_far if which else x_a], dst_ref=x1buf.at[j, which],
            send_sem=x1_s.at[j, which], recv_sem=x1_r.at[j, which],
            device_id=at(dp_=z_hi * 4 + x_a), device_id_type=MESH,
        )

    def x2_copy(j):
        return pltpu.make_async_remote_copy(
            src_ref=xs.at[j], dst_ref=x2buf.at[j],
            send_sem=x2_s.at[j], recv_sem=x2_r.at[j],
            device_id=at(dp_=z_hi * 4 + x_b), device_id_type=MESH,
        )

    def y_sum_copy(dy):
        to = lax.rem(ha + dy, 4)
        return pltpu.make_async_remote_copy(
            src_ref=cbuf.at[:, :, to], dst_ref=ybuf.at[dy - 1],
            send_sem=yy_s.at[dy - 1], recv_sem=yy_r.at[dy - 1],
            device_id=at(ha_=to), device_id_type=MESH,
        )

    def z_sum_copy(dz):
        return pltpu.make_async_remote_copy(
            src_ref=zbuf.at[:, lax.rem(zi + dz, 8)], dst_ref=zr.at[dz - 1],
            send_sem=zz_s.at[dz - 1], recv_sem=zz_r.at[dz - 1],
            device_id=z_device(dz), device_id_type=MESH,
        )

    def last_copy():
        return pltpu.make_async_remote_copy(
            src_ref=fbuf.at[:, 1 - core], dst_ref=f2, send_sem=fin_s.at[0], recv_sem=fin_r.at[0],
            device_id=at(wa_=mate), device_id_type=MESH,
        )

    def wide(value):
        return value.astype(F32)

    def add_mate(j):
        mate_copy(j).wait_recv()

        def add(at_x):
            for h in range(2):
                abuf[j, h, at_x] = (
                    wide(gbuf[2 * j + core, h, at_x]) + wide(rbuf[j, h, at_x])
                ).astype(BF)

        add(x_far)
        x1_copy(j, 1).start()
        add(x_a)
        x1_copy(j, 0).start()
        add(x_b)
        add(x)

    def add_x1(j):
        x1_copy(j, 1).wait_recv()
        for h in range(2):
            xs[j, h] = (wide(abuf[j, h, x_b]) + wide(x1buf[j, 1, h])).astype(BF)
        x2_copy(j).start()

    def add_x2(j):
        x1_copy(j, 0).wait_recv()
        x2_copy(j).wait_recv()
        for h in range(2):
            total = wide(abuf[j, h, x]) + wide(x1buf[j, 0, h]) + wide(x2buf[j, h])
            cbuf[j, h] = total.astype(BF).reshape(4, 48, HD)

    def send_y():
        for dy in (2, 1, 3):
            y_sum_copy(dy).start()

    pick = (lax.broadcasted_iota(jnp.int32, (128, 96), 0), lax.broadcasted_iota(jnp.int32, (128, 96), 1))

    def add_y():
        spread = (
            ((pick[0] & 7) < 6) & (pick[1] == (pick[0] >> 3) * 6 + (pick[0] & 7))
        ).astype(F32).astype(BF)
        for dy in (1, 2, 3):
            y_sum_copy(dy).wait_recv()
        for j in range(3):
            halves = []
            for h in range(2):
                total = wide(cbuf[j, h, ha])
                for n in range(3):
                    total = total + wide(ybuf[n, j, h])
                halves.append(total.astype(BF))
            rows = dot(spread, jnp.concatenate(halves, axis=0))
            zbuf[j] = rows.astype(BF).reshape(8, 16, HD)
        for dz in (4, 3, 5, 2, 6, 1, 7):
            z_sum_copy(dz).start()

    def add_z():
        for dz in range(1, 8):
            z_sum_copy(dz).wait_recv()
        for j in range(3):
            total = wide(zbuf[j, zi])
            for n in range(7):
                total = total + wide(zr[n, j])
            fbuf[j] = total.reshape(2, 8, HD)
        last_copy().start()

    def finish_weights():
        last_copy().wait_recv()
        for j in range(3):
            gws[2 * j + core] = fbuf[j, core]
            gws[2 * j + 1 - core] = f2[j]
        for h in range(HEADS):
            gw_out[:, h * HD : (h + 1) * HD] = head_value(lambda s: gws[(s + 1) % HEADS, 0:6, :], h)

    forward(HALO, qa0[0], qa0[1], kv0[0], kv0[1], None)
    weight_term(0)
    relay_kv(0)
    relay_kv(1)

    def forward_step(s, carry):
        @pl.when(s < HALO - 2)
        def _():
            relay_kv(s + 2)

        @pl.when(s == HALO - 3)
        def _():
            def own_qa(t, c):
                w_send(qa, wq_s, wq_r, t, 1)
                return c
            lax.fori_loop(0, HALO, own_qa, 0)

        @pl.when(s == 3)
        def _():
            relay_qa(0)
            relay_qa(1)

        @pl.when(s == 4)
        def _():
            relay_qa(2)

        w_wait(kv, wk_s, wk_r, s)
        forward(
            s, qa[s, 0, 1, 1], qa[s, 1, 1, 1],
            kv[s, 0].reshape(KEYS, HD), kv[s, 1].reshape(KEYS, HD), bias_row(s, False),
        )
        weight_term(s + 1)

        @pl.when(lax.rem(s, 2) == 0)
        def _():
            mate_copy(lax.div(s, 2)).start()

        @pl.when(lax.rem(s, 2) == 1)
        def _():
            add_mate(lax.div(s, 2))

        @pl.when((lax.rem(s, 2) == 0) & (s > 0))
        def _():
            add_x1(lax.div(s, 2) - 1)
        return carry

    lax.fori_loop(0, HALO, forward_step, 0)

    sb[1, 1] = stat[...].astype(BF)

    def sy_copy(r):
        return pltpu.make_async_remote_copy(
            src_ref=sb.at[1, 1], dst_ref=sb.at[r, 1], send_sem=sy_s.at[r // 2], recv_sem=sy_r.at[r // 2],
            device_id=at(ha_=ha_up if r == 2 else ha_down), device_id_type=MESH,
        )

    def sw_copy(r, c):
        return pltpu.make_async_remote_copy(
            src_ref=sb.at[r, 1], dst_ref=sb.at[r, c],
            send_sem=sw_s.at[r, c // 2], recv_sem=sw_r.at[r, c // 2],
            device_id=at(wa_=wa_right if c == 0 else wa_left), device_id_type=MESH,
        )

    def sw_send(r):
        for c in ANY_COLS:
            @pl.when(sends_to[c])
            def _(c=c):
                sw_copy(r, c).start()

    for r in (0, 2):
        sy_copy(r).start()
    sw_send(1)
    add_mate(2)
    relay_qa(3)
    relay_qa(4)
    add_x2(0)
    for r in (0, 2):
        sy_copy(r).wait_recv()
        sw_send(r)
    add_x1(2)

    chosen = (lax.broadcasted_iota(jnp.int32, (16, HD), 0), lax.broadcasted_iota(jnp.int32, (16, HD), 1))
    first = (chosen[0] & 7) * 3 + (chosen[0] >> 3) * 64
    take = ((chosen[1] >= first) & (chosen[1] < first + 3) & ((chosen[0] & 7) < 6)).astype(F32).astype(BF)

    own = dot_nt(take, sb[1, 1])
    backward(
        HALO, kv0[0], kv0[1], qa0[0], qa0[1], own[HALO : HALO + 1, :], own[8 + HALO : 9 + HALO, :]
    )
    add_x2(1)
    for c in ANY_COLS:
        @pl.when(gets_from[c])
        def _(c=c):
            for r in range(3):
                sw_copy(r, c).wait_recv()
    trow[...] = dot_nt(take, sb[...].reshape(KEYS, HD))
    add_x2(2)
    send_y()

    def backward_step(s, carry):
        w_wait(qa, wq_s, wq_r, s)
        backward(
            s, kv[s, 0, 1, 1], kv[s, 1, 1, 1], qa[s, 0].reshape(KEYS, HD), qa[s, 1].reshape(KEYS, HD),
            trow[pl.ds(s, 1), :] - bias_row(s, True), trow[pl.ds(s + 8, 1), :],
        )

        @pl.when(s == 0)
        def _():
            add_y()

        @pl.when(s == 2)
        def _():
            add_z()
        return carry

    lax.fori_loop(0, HALO, backward_step, 0)

    for h in range(HEADS):
        cols = slice(h * HD, (h + 1) * HD)
        gq_out[:, cols] = head_value(lambda s: res[0, s], h)
        gk_out[:, cols] = head_value(lambda s: res[1, s], h)
        gv_out[:, cols] = head_value(lambda s: res[2, s], h)
    finish_weights()

    def sent(s, carry):
        for r in (0, 2):
            y_copy(kv, yk_s, yk_r, s, r).wait_send()
            y_copy(qa, yq_s, yq_r, s, r).wait_send()
        for c in ANY_COLS:
            @pl.when(sends_to[c])
            def _(c=c):
                for r in range(3):
                    w_copy(kv, wk_s, wk_r, s, r, c).wait_send()
                    w_copy(qa, wq_s, wq_r, s, r, c).wait_send()
        return carry

    lax.fori_loop(0, HALO, sent, 0)
    for r in (0, 2):
        sy_copy(r).wait_send()
    for c in ANY_COLS:
        @pl.when(sends_to[c])
        def _(c=c):
            for r in range(3):
                sw_copy(r, c).wait_send()
    for j in range(3):
        mate_copy(j).wait_send()
        x1_copy(j, 0).wait_send()
        x1_copy(j, 1).wait_send()
        x2_copy(j).wait_send()
    for dy in (1, 2, 3):
        y_sum_copy(dy).wait_send()
    for dz in range(1, 8):
        z_sum_copy(dz).wait_send()
    last_copy().wait_send()


def shards(queries, key_tiles, value_tiles, out_grad, w_out, reaches):
    dma = pltpu.SemaphoreType.DMA
    vm = pltpu.VMEM
    shapes = [
        vm((TILE, HQ), BF), vm((TILE, HQ), BF), vm((TILE, HQ), BF), vm((TILE, D), BF), vm((D, HQ), BF),
        vm((TILE, HQ), BF), vm((D, TILE), BF),
        vm((HALO, 2, 3, 3, TILE, HD), BF), vm((HALO, 2, 3, 3, TILE, HD), BF),
        vm((2, TILE, HD), BF), vm((2, TILE, HD), BF),
        vm((TILE, HD), F32), vm((3, 3, TILE, HD), BF), vm((16, KEYS), F32),
        vm((TILE, KEYS), F32), vm((TILE, KEYS), F32), vm((TILE, KEYS), BF), vm((TILE, KEYS), BF),
        vm((TILE, HD), BF), vm((3, HEADS, TILE, HD), BF),
        vm((6, 2, 4, 192, HD), BF), vm((3, 2, 4, 192, HD), BF), vm((3, 2, 4, 192, HD), BF),
        vm((3, 2, 2, 192, HD), BF), vm((3, 2, 192, HD), BF), vm((3, 2, 192, HD), BF),
        vm((3, 2, 4, 48, HD), BF), vm((3, 3, 2, 48, HD), BF),
        vm((3, 8, 16, HD), BF), vm((7, 3, 16, HD), BF),
        vm((3, 2, 8, HD), F32), vm((3, 8, HD), F32), vm((6, 8, HD), F32),
        dma((5,)),
    ]
    for extent in ((HALO, 2), (HALO, 2), (HALO, 3, 2), (HALO, 3, 2), (2,), (3, 2), (3,), (3, 2), (3,), (3,), (7,), (1,)):
        shapes += [dma(extent), dma(extent)]
    tile = jax.ShapeDtypeStruct((TILE, HQ), BF)
    anywhere = pl.BlockSpec(memory_space=pl.ANY)
    inside = pl.BlockSpec(memory_space=pltpu.VMEM)
    gq, gk, gv, gw = pl.pallas_call(
        kernel,
        out_shape=(tile, tile, tile, jax.ShapeDtypeStruct((6, HQ), F32)),
        in_specs=[pl.BlockSpec(memory_space=pltpu.SMEM)] + [anywhere] * 5,
        out_specs=(inside,) * 4,
        scratch_shapes=shapes,
        compiler_params=pltpu.CompilerParams(collective_id=0, has_side_effects=True),
    )(
        reaches,
        queries.reshape(TILE, HQ),
        key_tiles.reshape(TILE, HQ),
        value_tiles.reshape(TILE, HQ),
        out_grad.reshape(TILE, D),
        w_out,
    )
    return gq.reshape(queries.shape), gk.reshape(queries.shape), gv.reshape(queries.shape), gw


def solution(mesh):
    tiles = P("dp", None, "ha", "wa", None, None)
    return jax.shard_map(
        shards,
        mesh=mesh,
        in_specs=(tiles, tiles, tiles, tiles, P(), P()),
        out_specs=(tiles, tiles, tiles, P(("dp", "ha", "wa"), None)),
        check_vma=False,
    )
```

time: 193 us -> 75 us (0.39)
  Pallas kernels: 0 us -> 67.9 us
  waiting for transfers between devices: 62 us -> 0 us
  starting transfers between devices: 45.7 us -> 0 us
  matrix products: 31.4 us -> 0 us
  other arithmetic: 20.7 us -> 0 us
  between operations: 16.4 us -> 0.64 us
  local copies, waits for them, and re-layouts: 15.2 us -> 6.25 us
    pallas_call x0 -> x1, Pallas kernels: none -> 67.9 us  [shards(): pl.pallas_call(kernel, out_shape=(tile, tile, tile, jax.ShapeDtypeStruct(...]
    ppermute x8 -> x0, waiting for transfers between devices: 45.9 us -> none  [the longest x4 35 us: shifted(): return lax.ppermute(block, axis, route)]
    dot_general x38 -> x0, matrix products: 31.4 us -> none  [the longest x6 8.88 us: shards(): jnp.dot(grad_scores, key_head, preferred_element_type=jnp.float32)]
    ppermute x8 -> x0, starting transfers between devices: 26.3 us -> none  [the longest x4 12.7 us: shifted(): return lax.ppermute(block, axis, route)]
    all_to_all x2 -> x0, starting transfers between devices: 19.4 us -> none  [the longest x1 9.75 us: sum_at_owner(): parts = lax.all_to_all(split_up(array, dim, size), axis, 0, 0, tiled=True)]
    all_to_all x2 -> x0, waiting for transfers between devices: 16.1 us -> none  [the longest x1 16.1 us: sum_at_owner(): parts = lax.all_to_all(split_up(array, dim, size), axis, 0, 0, tiled=True)]
    and x12 -> x0, other arithmetic: 8.05 us -> none  [the longest x9 4.29 us: tile_allowed(): time_ok[:, :, None, None] & row_ok[None, None, :, None]]
    convert_element_type x3 -> x0, local copies, waits for them, and re-layouts: 5.7 us -> none  [the longest x1 4.37 us: shards(): coarse = sent_and_summed(lax.dot_general(grad_rows, attended, (((0,), (0,...]
  transfers between devices with their start and end apart: 10 -> 0, of which waited for: 4 -> 0; matrix products, arithmetic and copies ran while one was open for 21% -> 0% of each run, Pallas kernels for 0% -> 0%
where the time goes in v1:
time: 75 us; the launch traced here: 74.8 us
  Pallas kernels  67.9 us (91%)
  local copies, waits for them, and re-layouts  6.25 us (8%)
    pallas_call x1, Pallas kernels, shards(): pl.pallas_call(kernel, out_shape=(tile, tile, tile, jax.ShapeDtypeStruct(...  67.9 us
    unnamed x4, local copies, waits for them, and re-layouts  6.25 us

profile of v1, /device:TPU:1, one launch (start us, length us, event | category | flops | bytes accessed | tf_op | source)
XLA Modules:
  0.0 74.8 jit_solution(15854887595673738192)
XLA Ops:
  0.6 67.9 %shard_map.93 = (bf16[144,768]{1,0:T(8,128)(2,1)}, bf16[144,768]{1,0:T(8,128)(2,1)}, bf16[144,768]{1,0:T(8,128)(2,1)}, f32[6,768]{1,0:T(8,128)}) custom-call(s32[6,6]{1,0:T(8,128)} %reach.1, bf16[144,768]{1,0:T(8,128)(2,1)} %bitcast.11, bf16[144,768]{1,0:T(8,128)(2,1)} %bitcast.12, bf16[144,768]{1,0:T(8,128)(2,1)} %bitcast.13, bf16[144,1536]{1,0:T(8,128)(2,1)} %bitcast.7, ...), custom_call_target="tpu_custom_call" | custom-call | tf_op jit(solution)/shard_map/pallas_call | solution.py:610
  68.5 1.6 %copy.14 = bf16[1,1,1,1,144,768]{5,4,3,2,1,0:T(8,128)(2,1)} copy(bf16[1,1,1,1,144,768]{5,4,3,2,1,0:T(8,128)(2,1)} %bitcast.10) | data formatting | bytes 442368
  70.1 1.6 %copy.15 = bf16[1,1,1,1,144,768]{5,4,3,2,1,0:T(8,128)(2,1)} copy(bf16[1,1,1,1,144,768]{5,4,3,2,1,0:T(8,128)(2,1)} %bitcast.9) | data formatting | bytes 442368
  71.8 1.6 %copy.16 = bf16[1,1,1,1,144,768]{5,4,3,2,1,0:T(8,128)(2,1)} copy(bf16[1,1,1,1,144,768]{5,4,3,2,1,0:T(8,128)(2,1)} %bitcast.8) | data formatting | bytes 442368
  73.4 1.3 %copy.17 = f32[6,768]{1,0:T(8,128)} copy(f32[6,768]{1,0:T(8,128)} %get-tuple-element.19) | data formatting | bytes 36864

commit v2 on v1

--- a/solution.py
+++ b/solution.py
@@ -17,6 +17,7 @@
 D = 1536
 SCALE = 1.0 / math.sqrt(HD)
 ROWS = 16
+FORWARD_UNROLL = 9
 BF = jnp.bfloat16
 F32 = jnp.float32
 ANY_COLS = (0, 2)
@@ -31,9 +32,9 @@
 
 
 def kernel(
-    reach, q_in, k_in, v_in, og_in, w_in,
-    gq_out, gk_out, gv_out, gw_out,
-    q_v, k_v, v_v, og_v, w_v, a_v, ogt, kv, qa, kv0, qa0, stat, sb, trow,
+    reach_in, q_in, k_in, v_in, og_in, w_in,
+    grads_out, gw_out,
+    reach, q_v, k_v, v_v, og_v, w_v, a_v, ogt, kv, qa, kv0, qa0, stat, sb, trow,
     s_buf, dp_buf, p_buf, ds_buf, att_buf, res,
     gbuf, rbuf, abuf, x1buf, xs, x2buf, cbuf, ybuf, zbuf, zr, fbuf, f2, gws,
     in_sem, yk_s, yk_r, yq_s, yq_r, wk_s, wk_r, wq_s, wq_r, sy_s, sy_r, sw_s, sw_r,
@@ -59,6 +60,15 @@
     def at(dp_=dp, ha_=ha, wa_=wa):
         return (dp_, ha_, wa_)
 
+    loads = [
+        pltpu.make_async_copy(src, dst, in_sem.at[n])
+        for n, (src, dst) in enumerate(
+            ((k_in, k_v), (v_in, v_v), (q_in, q_v), (og_in, og_v), (w_in, w_v), (reach_in, reach))
+        )
+    ]
+    for n in (5, 0, 1, 3, 4, 2):
+        loads[n].start()
+
     barrier = pltpu.get_barrier_semaphore()
 
     def greet(device):
@@ -86,22 +96,6 @@
     @pl.when(far_left)
     def _():
         greet(at(wa_=wa - 1))
-
-    loads = [
-        pltpu.make_async_copy(src, dst, in_sem.at[n])
-        for n, (src, dst) in enumerate(
-            ((k_in, k_v), (v_in, v_v), (q_in, q_v), (og_in, og_v), (w_in, w_v))
-        )
-    ]
-    for load in loads:
-        load.start()
-
-    zero_head = jnp.int32(0)
-    for n in reversed(range(HEADS)):
-        total = reach[n, 0]
-        for t in range(1, 6):
-            total = total + reach[n, t]
-        zero_head = jnp.where(total == 0, n, zero_head)
 
     def columns(ref, head):
         return ref[:, head * HD : (head + 1) * HD]
@@ -143,14 +137,26 @@
         for r in range(3):
             sb[r, 2] = jnp.zeros((TILE, HD), BF)
 
+    loads[5].wait()
+
+    zero_head = jnp.int32(0)
+    for n in reversed(range(HEADS)):
+        total = reach[n, 0]
+        for t in range(1, 6):
+            total = total + reach[n, t]
+        zero_head = jnp.where(total == 0, n, zero_head)
+
     loads[0].wait()
     loads[1].wait()
 
-    for s in range(HALO):
-        kv[s, 0, 1, 1] = slot_columns(k_v, s)
-        kv[s, 1, 1, 1] = slot_columns(v_v, s)
-    kv0[0] = zero_columns(k_v)
-    kv0[1] = zero_columns(v_v)
+    def place_own_kv():
+        for s in range(HALO):
+            kv[s, 0, 1, 1] = slot_columns(k_v, s)
+            kv[s, 1, 1, 1] = slot_columns(v_v, s)
+        kv0[0] = zero_columns(k_v)
+        kv0[1] = zero_columns(v_v)
+
+    place_own_kv()
 
     ha_up = lax.rem(ha + 3, 4)
     ha_down = lax.rem(ha + 1, 4)
@@ -198,7 +204,10 @@
     def relay_qa(s):
         relay(qa, yq_s, yq_r, wq_s, wq_r, s)
 
-    pl.semaphore_wait(barrier, 13 + (far_right | far_left).astype(jnp.int32))
+    def wait_barrier():
+        pl.semaphore_wait(barrier, 13 + (far_right | far_left).astype(jnp.int32))
+
+    wait_barrier()
 
     def first_kv(s, carry):
         for r in (0, 2):
@@ -208,24 +217,35 @@
 
     lax.fori_loop(0, HALO, first_kv, 0)
 
-    loads[2].wait()
-    loads[3].wait()
-    loads[4].wait()
-    a_v[...] = dot(og_v[...], w_v[...]).astype(BF)
-
-    for s in range(HALO):
-        qa[s, 0, 1, 1] = slot_columns(q_v, s)
-        qa[s, 1, 1, 1] = slot_columns(a_v, s)
-        for r in (0, 2):
-            y_copy(qa, yq_s, yq_r, s, r).start()
-    qa0[0] = zero_columns(q_v)
-    qa0[1] = zero_columns(a_v)
+    def wait_loads():
+        loads[2].wait()
+        loads[3].wait()
+        loads[4].wait()
+
+    def amat():
+        a_v[...] = dot(og_v[...], w_v[...]).astype(BF)
+
+    def place_own_qa():
+        for s in range(HALO):
+            qa[s, 0, 1, 1] = slot_columns(q_v, s)
+            qa[s, 1, 1, 1] = slot_columns(a_v, s)
+            for r in (0, 2):
+                y_copy(qa, yq_s, yq_r, s, r).start()
+        qa0[0] = zero_columns(q_v)
+        qa0[1] = zero_columns(a_v)
 
     eye = (
         lax.broadcasted_iota(jnp.int32, (HD, HD), 0) == lax.broadcasted_iota(jnp.int32, (HD, HD), 1)
     ).astype(F32).astype(BF)
-    for t in range(D // HD):
-        ogt[t * HD : (t + 1) * HD, :] = dot_nt(eye, og_v[:, t * HD : (t + 1) * HD]).astype(BF)
+
+    def transpose_og():
+        for t in range(D // HD):
+            ogt[t * HD : (t + 1) * HD, :] = dot_nt(eye, og_v[:, t * HD : (t + 1) * HD]).astype(BF)
+
+    wait_loads()
+    amat()
+    place_own_qa()
+    transpose_og()
 
     stat[...] = jnp.zeros((TILE, HD), F32)
     lane = lax.broadcasted_iota(jnp.int32, (ROWS, HD), 1)
@@ -285,8 +305,8 @@
             stat[rows, :] = block
             return carry
 
-        lax.fori_loop(0, TILE // ROWS, rows_step, 0)
-        att_buf[...] = dot(p_buf[:, :n], v).astype(BF)
+        lax.fori_loop(0, TILE // ROWS, rows_step, 0, unroll=FORWARD_UNROLL if n == KEYS else True)
+        att_buf[lax.rem(slot + 1, 2)] = dot(p_buf[:, :n], v).astype(BF)
         res[0, slot] = (dot(ds_buf[:, :n], k) * SCALE).astype(BF)
 
     def backward(slot, k, v, q, a, lse_row, delta_row):
@@ -305,13 +325,12 @@
         res[2, slot] = dot(p_buf[:, :n], a).astype(BF)
         res[1, slot] = (dot(ds_buf[:, :n], q) * SCALE).astype(BF)
 
-    def weight_term(index):
-        def step(t, carry):
-            rows = pl.ds(pl.multiple_of(t * 192, 192), 192)
-            gbuf[index, lax.div(t, 4), lax.rem(t, 4)] = dot(ogt[rows, :], att_buf[...]).astype(BF)
-            return carry
-
-        lax.fori_loop(0, 8, step, 0)
+    def weight_term(pair):
+        attended = jnp.concatenate([att_buf[0], att_buf[1]], axis=1)
+        for t in range(8):
+            both = dot(ogt[t * 192 : (t + 1) * 192, :], attended).astype(BF)
+            gbuf[2 * pair, t // 4, t % 4] = both[:, :HD]
+            gbuf[2 * pair + 1, t // 4, t % 4] = both[:, HD:]
 
     def mate_copy(j):
         return pltpu.make_async_remote_copy(
@@ -333,11 +352,11 @@
             device_id=at(dp_=z_hi * 4 + x_b), device_id_type=MESH,
         )
 
-    def y_sum_copy(dy):
+    def y_sum_copy(j, dy):
         to = lax.rem(ha + dy, 4)
         return pltpu.make_async_remote_copy(
-            src_ref=cbuf.at[:, :, to], dst_ref=ybuf.at[dy - 1],
-            send_sem=yy_s.at[dy - 1], recv_sem=yy_r.at[dy - 1],
+            src_ref=cbuf.at[j, :, to], dst_ref=ybuf.at[dy - 1, j],
+            send_sem=yy_s.at[j, dy - 1], recv_sem=yy_r.at[j, dy - 1],
             device_id=at(ha_=to), device_id_type=MESH,
         )
 
@@ -385,28 +404,28 @@
         for h in range(2):
             total = wide(abuf[j, h, x]) + wide(x1buf[j, 0, h]) + wide(x2buf[j, h])
             cbuf[j, h] = total.astype(BF).reshape(4, 48, HD)
-
-    def send_y():
         for dy in (2, 1, 3):
-            y_sum_copy(dy).start()
+            y_sum_copy(j, dy).start()
 
     pick = (lax.broadcasted_iota(jnp.int32, (128, 96), 0), lax.broadcasted_iota(jnp.int32, (128, 96), 1))
 
-    def add_y():
-        spread = (
-            ((pick[0] & 7) < 6) & (pick[1] == (pick[0] >> 3) * 6 + (pick[0] & 7))
-        ).astype(F32).astype(BF)
+    spread = (
+        ((pick[0] & 7) < 6) & (pick[1] == (pick[0] >> 3) * 6 + (pick[0] & 7))
+    ).astype(F32).astype(BF)
+
+    def add_y(j):
         for dy in (1, 2, 3):
-            y_sum_copy(dy).wait_recv()
-        for j in range(3):
-            halves = []
-            for h in range(2):
-                total = wide(cbuf[j, h, ha])
-                for n in range(3):
-                    total = total + wide(ybuf[n, j, h])
-                halves.append(total.astype(BF))
-            rows = dot(spread, jnp.concatenate(halves, axis=0))
-            zbuf[j] = rows.astype(BF).reshape(8, 16, HD)
+            y_sum_copy(j, dy).wait_recv()
+        halves = []
+        for h in range(2):
+            total = wide(cbuf[j, h, ha])
+            for n in range(3):
+                total = total + wide(ybuf[n, j, h])
+            halves.append(total.astype(BF))
+        rows = dot(spread, jnp.concatenate(halves, axis=0))
+        zbuf[j] = rows.astype(BF).reshape(8, 16, HD)
+
+    def send_z():
         for dz in (4, 3, 5, 2, 6, 1, 7):
             z_sum_copy(dz).start()
 
@@ -428,52 +447,51 @@
         for h in range(HEADS):
             gw_out[:, h * HD : (h + 1) * HD] = head_value(lambda s: gws[(s + 1) % HEADS, 0:6, :], h)
 
+    def own_qa():
+        def step(t, c):
+            w_send(qa, wq_s, wq_r, t, 1)
+            return c
+
+        lax.fori_loop(0, HALO, step, 0)
+
+    def hooked(s, hooks):
+        for n, ops in hooks.items():
+            @pl.when(s == n)
+            def _(ops=ops):
+                for op, *args in ops:
+                    op(*args)
+
+    def pair_done(pair):
+        weight_term(pair)
+        mate_copy(pair).start()
+
     forward(HALO, qa0[0], qa0[1], kv0[0], kv0[1], None)
-    weight_term(0)
     relay_kv(0)
     relay_kv(1)
 
     def forward_step(s, carry):
-        @pl.when(s < HALO - 2)
-        def _():
-            relay_kv(s + 2)
-
-        @pl.when(s == HALO - 3)
-        def _():
-            def own_qa(t, c):
-                w_send(qa, wq_s, wq_r, t, 1)
-                return c
-            lax.fori_loop(0, HALO, own_qa, 0)
-
-        @pl.when(s == 3)
-        def _():
-            relay_qa(0)
-            relay_qa(1)
-
-        @pl.when(s == 4)
-        def _():
-            relay_qa(2)
-
+        hooked(s, BEFORE_FORWARD)
         w_wait(kv, wk_s, wk_r, s)
         forward(
             s, qa[s, 0, 1, 1], qa[s, 1, 1, 1],
             kv[s, 0].reshape(KEYS, HD), kv[s, 1].reshape(KEYS, HD), bias_row(s, False),
         )
-        weight_term(s + 1)
-
-        @pl.when(lax.rem(s, 2) == 0)
-        def _():
-            mate_copy(lax.div(s, 2)).start()
-
-        @pl.when(lax.rem(s, 2) == 1)
-        def _():
-            add_mate(lax.div(s, 2))
-
-        @pl.when((lax.rem(s, 2) == 0) & (s > 0))
-        def _():
-            add_x1(lax.div(s, 2) - 1)
+        hooked(s, AFTER_FORWARD)
         return carry
 
+    BEFORE_FORWARD = {
+        0: [(relay_kv, 2)],
+        1: [(relay_kv, 3)],
+        2: [(relay_kv, 4), (own_qa,)],
+        3: [(relay_qa, 0)],
+        4: [(relay_qa, 1)],
+    }
+    AFTER_FORWARD = {
+        0: [(pair_done, 0)],
+        2: [(pair_done, 1)],
+        3: [(add_mate, 0)],
+        4: [(pair_done, 2)],
+    }
     lax.fori_loop(0, HALO, forward_step, 0)
 
     sb[1, 1] = stat[...].astype(BF)
@@ -500,32 +518,41 @@
     for r in (0, 2):
         sy_copy(r).start()
     sw_send(1)
-    add_mate(2)
-    relay_qa(3)
-    relay_qa(4)
-    add_x2(0)
-    for r in (0, 2):
-        sy_copy(r).wait_recv()
-        sw_send(r)
-    add_x1(2)
+    relay_qa(2)
+    add_mate(1)
+    add_x1(0)
 
     chosen = (lax.broadcasted_iota(jnp.int32, (16, HD), 0), lax.broadcasted_iota(jnp.int32, (16, HD), 1))
     first = (chosen[0] & 7) * 3 + (chosen[0] >> 3) * 64
     take = ((chosen[1] >= first) & (chosen[1] < first + 3) & ((chosen[0] & 7) < 6)).astype(F32).astype(BF)
 
+    relay_qa(3)
     own = dot_nt(take, sb[1, 1])
     backward(
         HALO, kv0[0], kv0[1], qa0[0], qa0[1], own[HALO : HALO + 1, :], own[8 + HALO : 9 + HALO, :]
     )
-    add_x2(1)
-    for c in ANY_COLS:
-        @pl.when(gets_from[c])
-        def _(c=c):
-            for r in range(3):
-                sw_copy(r, c).wait_recv()
+    add_mate(2)
+
+    def relay_stats():
+        for r in (0, 2):
+            sy_copy(r).wait_recv()
+            sw_send(r)
+
+    relay_stats()
+    relay_qa(4)
+    add_x1(1)
+    add_x2(0)
+
+    def wait_stats():
+        for c in ANY_COLS:
+            @pl.when(gets_from[c])
+            def _(c=c):
+                for r in range(3):
+                    sw_copy(r, c).wait_recv()
+
+    add_x1(2)
+    wait_stats()
     trow[...] = dot_nt(take, sb[...].reshape(KEYS, HD))
-    add_x2(2)
-    send_y()
 
     def backward_step(s, carry):
         w_wait(qa, wq_s, wq_r, s)
@@ -533,23 +560,24 @@
             s, kv[s, 0, 1, 1], kv[s, 1, 1, 1], qa[s, 0].reshape(KEYS, HD), qa[s, 1].reshape(KEYS, HD),
             trow[pl.ds(s, 1), :] - bias_row(s, True), trow[pl.ds(s + 8, 1), :],
         )
-
-        @pl.when(s == 0)
-        def _():
-            add_y()
-
-        @pl.when(s == 2)
-        def _():
-            add_z()
+        hooked(s, AFTER_BACKWARD)
         return carry
 
+    AFTER_BACKWARD = {
+        0: [(add_x2, 1), (add_x2, 2)],
+        1: [(add_y, 0)],
+        2: [(add_y, 1), (add_y, 2), (send_z,)],
+    }
     lax.fori_loop(0, HALO, backward_step, 0)
 
-    for h in range(HEADS):
-        cols = slice(h * HD, (h + 1) * HD)
-        gq_out[:, cols] = head_value(lambda s: res[0, s], h)
-        gk_out[:, cols] = head_value(lambda s: res[1, s], h)
-        gv_out[:, cols] = head_value(lambda s: res[2, s], h)
+    def place_outputs():
+        for h in range(HEADS):
+            cols = slice(h * HD, (h + 1) * HD)
+            for n in range(3):
+                grads_out[n, :, cols] = head_value(lambda s: res[n, s], h)
+
+    place_outputs()
+    add_z()
     finish_weights()
 
     def sent(s, carry):
@@ -577,41 +605,53 @@
         x1_copy(j, 0).wait_send()
         x1_copy(j, 1).wait_send()
         x2_copy(j).wait_send()
-    for dy in (1, 2, 3):
-        y_sum_copy(dy).wait_send()
+    for j in range(3):
+        for dy in (1, 2, 3):
+            y_sum_copy(j, dy).wait_send()
     for dz in range(1, 8):
         z_sum_copy(dz).wait_send()
     last_copy().wait_send()
+
+
+def put_out(grads, gw, gq_out, gk_out, gv_out, gw_out, sem):
+    copies = [
+        pltpu.make_async_copy(grads.at[n], ref, sem.at[n]) for n, ref in enumerate((gq_out, gk_out, gv_out))
+    ]
+    copies.append(pltpu.make_async_copy(gw, gw_out, sem.at[3]))
+    for copy in copies:
+        copy.start()
+    for copy in copies:
+        copy.wait()
 
 
 def shards(queries, key_tiles, value_tiles, out_grad, w_out, reaches):
     dma = pltpu.SemaphoreType.DMA
     vm = pltpu.VMEM
     shapes = [
+        pltpu.SMEM((HEADS, 6), jnp.int32),
         vm((TILE, HQ), BF), vm((TILE, HQ), BF), vm((TILE, HQ), BF), vm((TILE, D), BF), vm((D, HQ), BF),
         vm((TILE, HQ), BF), vm((D, TILE), BF),
         vm((HALO, 2, 3, 3, TILE, HD), BF), vm((HALO, 2, 3, 3, TILE, HD), BF),
         vm((2, TILE, HD), BF), vm((2, TILE, HD), BF),
         vm((TILE, HD), F32), vm((3, 3, TILE, HD), BF), vm((16, KEYS), F32),
         vm((TILE, KEYS), F32), vm((TILE, KEYS), F32), vm((TILE, KEYS), BF), vm((TILE, KEYS), BF),
-        vm((TILE, HD), BF), vm((3, HEADS, TILE, HD), BF),
+        vm((2, TILE, HD), BF), vm((3, HEADS, TILE, HD), BF),
         vm((6, 2, 4, 192, HD), BF), vm((3, 2, 4, 192, HD), BF), vm((3, 2, 4, 192, HD), BF),
         vm((3, 2, 2, 192, HD), BF), vm((3, 2, 192, HD), BF), vm((3, 2, 192, HD), BF),
         vm((3, 2, 4, 48, HD), BF), vm((3, 3, 2, 48, HD), BF),
         vm((3, 8, 16, HD), BF), vm((7, 3, 16, HD), BF),
         vm((3, 2, 8, HD), F32), vm((3, 8, HD), F32), vm((6, 8, HD), F32),
-        dma((5,)),
+        dma((6,)),
     ]
-    for extent in ((HALO, 2), (HALO, 2), (HALO, 3, 2), (HALO, 3, 2), (2,), (3, 2), (3,), (3, 2), (3,), (3,), (7,), (1,)):
+    for extent in ((HALO, 2), (HALO, 2), (HALO, 3, 2), (HALO, 3, 2), (2,), (3, 2), (3,), (3, 2), (3,), (3, 3), (7,), (1,)):
         shapes += [dma(extent), dma(extent)]
-    tile = jax.ShapeDtypeStruct((TILE, HQ), BF)
     anywhere = pl.BlockSpec(memory_space=pl.ANY)
     inside = pl.BlockSpec(memory_space=pltpu.VMEM)
-    gq, gk, gv, gw = pl.pallas_call(
+    grads, gw = pl.pallas_call(
         kernel,
-        out_shape=(tile, tile, tile, jax.ShapeDtypeStruct((6, HQ), F32)),
-        in_specs=[pl.BlockSpec(memory_space=pltpu.SMEM)] + [anywhere] * 5,
-        out_specs=(inside,) * 4,
+        out_shape=(pltpu.VMEM((3, TILE, HQ), BF), pltpu.VMEM((6, HQ), F32)),
+        in_specs=[anywhere] * 6,
+        out_specs=(inside,) * 2,
         scratch_shapes=shapes,
         compiler_params=pltpu.CompilerParams(collective_id=0, has_side_effects=True),
     )(
@@ -622,6 +662,14 @@
         out_grad.reshape(TILE, D),
         w_out,
     )
+    tile = jax.ShapeDtypeStruct((TILE, HQ), BF)
+    gq, gk, gv, gw = pl.pallas_call(
+        put_out,
+        out_shape=(tile, tile, tile, jax.ShapeDtypeStruct((6, HQ), F32)),
+        in_specs=[inside] * 2,
+        out_specs=(anywhere,) * 4,
+        scratch_shapes=[dma((4,))],
+    )(*(pltpu.with_memory_space_constraint(value, pltpu.VMEM) for value in (grads, gw)))
     return gq.reshape(queries.shape), gk.reshape(queries.shape), gv.reshape(queries.shape), gw
 
 

time: 75 us -> 52.2 us (0.70)
  Pallas kernels: 67.9 us -> 51.4 us
  local copies, waits for them, and re-layouts: 6.25 us -> 0 us
    pallas_call x1 -> x2, Pallas kernels: 67.9 us -> 51.4 us  [the longest x1 50.6 us: shards(): pl.pallas_call(kernel, out_shape=(pltpu.VMEM((3, TILE, HQ), BF), pltpu.VM...]
    unnamed x4 -> x0, local copies, waits for them, and re-layouts: 6.25 us -> none
where the time goes in v2:
time: 52.2 us; the launch traced here: 52.1 us
  Pallas kernels  51.4 us (98%)
  between operations  0.64 us (1%)
    pallas_call x1, Pallas kernels, shards(): pl.pallas_call(kernel, out_shape=(pltpu.VMEM((3, TILE, HQ), BF), pltpu.VM...  50.6 us

profile of v2, /device:TPU:1, one launch (start us, length us, event | category | flops | bytes accessed | tf_op | source)
XLA Modules:
  0.0 52.1 jit_solution(1353536960128003017)
XLA Ops:
  0.6 50.6 %shard_map.93 = (bf16[3,144,768]{2,1,0:T(8,128)(2,1)S(1)}, f32[6,768]{1,0:T(8,128)S(1)}) custom-call(s32[6,6]{1,0:T(8,128)} %reach_in.1, bf16[144,768]{1,0:T(8,128)(2,1)} %bitcast.8, bf16[144,768]{1,0:T(8,128)(2,1)} %bitcast.9, bf16[144,768]{1,0:T(8,128)(2,1)} %bitcast.10, bf16[144,1536]{1,0:T(8,128)(2,1)} %bitcast.7, bf16[1536,768]{1,0:T(8,128)(2,1)} %w_in.1), custom_call_target="tpu_custom_call" | custom-call | tf_op jit(solution)/shard_map/pallas_call | solution.py:650
  51.2 0.9 %shard_map.94 = (bf16[144,768]{1,0:T(8,128)(2,1)}, bf16[144,768]{1,0:T(8,128)(2,1)}, bf16[144,768]{1,0:T(8,128)(2,1)}, f32[6,768]{1,0:T(8,128)}) custom-call(bf16[3,144,768]{2,1,0:T(8,128)(2,1)S(1)} %get-tuple-element.10.grads, f32[6,768]{1,0:T(8,128)S(1)} %get-tuple-element.11.gw), custom_call_target="tpu_custom_call" | custom-call | tf_op jit(solution)/shard_map/pallas_call | solution.py:666

commit v3 on v2

--- a/solution.py
+++ b/solution.py
@@ -36,9 +36,9 @@
     grads_out, gw_out,
     reach, q_v, k_v, v_v, og_v, w_v, a_v, ogt, kv, qa, kv0, qa0, stat, sb, trow,
     s_buf, dp_buf, p_buf, ds_buf, att_buf, res,
-    gbuf, rbuf, abuf, x1buf, xs, x2buf, cbuf, ybuf, zbuf, zr, fbuf, f2, gws,
+    gbuf, rbuf, abuf, x1buf, xs, x2buf, cbuf, ybuf, zbuf, zr, gws,
     in_sem, yk_s, yk_r, yq_s, yq_r, wk_s, wk_r, wq_s, wq_r, sy_s, sy_r, sw_s, sw_r,
-    dd_s, dd_r, x1_s, x1_r, x2_s, x2_r, yy_s, yy_r, zz_s, zz_r, fin_s, fin_r,
+    dd_s, dd_r, x1_s, x1_r, x2_s, x2_r, yy_s, yy_r, zz_s, zz_r,
 ):
     dp = lax.axis_index("dp")
     ha = lax.axis_index("ha")
@@ -80,12 +80,15 @@
     greet(at(dp_=z_hi * 4 + x_one))
     greet(at(dp_=z_hi * 4 + x_three))
 
-    def z_device(dz):
+    def z_target(shift, other):
+        zl = lax.rem(z_lo + shift, 4)
+        to_core = 1 - core if other else core
+        return at(dp_=core * 4 + x, wa_=zl * 2 + to_core)
+
+    for dz in range(1, 8):
         zt = lax.rem(zi + dz, 8)
-        return at(dp_=lax.div(zt, 4) * 4 + x, wa_=lax.rem(zt, 4) * 2 + core)
-
-    for dz in range(1, 8):
-        greet(z_device(dz))
+        greet(at(dp_=lax.div(zt, 4) * 4 + x, wa_=lax.rem(zt, 4) * 2 + z_hi))
+    own_z = z_hi == core
     far_right = (core == 1) & has_right
     far_left = (core == 0) & has_left
 
@@ -166,14 +169,14 @@
     def y_copy(buf, send, recv, s, r):
         return pltpu.make_async_remote_copy(
             src_ref=buf.at[s, :, 1, 1], dst_ref=buf.at[s, :, r, 1],
-            send_sem=send.at[s, r // 2], recv_sem=recv.at[s, r // 2],
+            send_sem=send.at[r // 2], recv_sem=recv.at[s, r // 2],
             device_id=at(ha_=ha_up if r == 2 else ha_down), device_id_type=MESH,
         )
 
     def w_copy(buf, send, recv, s, r, c):
         return pltpu.make_async_remote_copy(
             src_ref=buf.at[s, :, r, 1], dst_ref=buf.at[s, :, r, c],
-            send_sem=send.at[s, r, c // 2], recv_sem=recv.at[s, r, c // 2],
+            send_sem=send.at[c // 2], recv_sem=recv.at[s, c // 2],
             device_id=at(wa_=wa_right if c == 0 else wa_left), device_id_type=MESH,
         )
 
@@ -195,8 +198,7 @@
         for c in ANY_COLS:
             @pl.when(gets_from[c])
             def _(c=c):
-                for r in range(3):
-                    w_copy(buf, send, recv, s, r, c).wait_recv()
+                pltpu.make_async_copy(buf.at[s, :, :, 1], buf.at[s, :, :, c], recv.at[s, c // 2]).wait()
 
     def relay_kv(s):
         relay(kv, yk_s, yk_r, wk_s, wk_r, s)
@@ -205,7 +207,7 @@
         relay(qa, yq_s, yq_r, wq_s, wq_r, s)
 
     def wait_barrier():
-        pl.semaphore_wait(barrier, 13 + (far_right | far_left).astype(jnp.int32))
+        pl.semaphore_wait(barrier, 14 - 2 * own_z.astype(jnp.int32) + (far_right | far_left).astype(jnp.int32))
 
     wait_barrier()
 
@@ -325,125 +327,150 @@
         res[2, slot] = dot(p_buf[:, :n], a).astype(BF)
         res[1, slot] = (dot(ds_buf[:, :n], q) * SCALE).astype(BF)
 
-    def weight_term(pair):
-        attended = jnp.concatenate([att_buf[0], att_buf[1]], axis=1)
+    GROUPS = ((0, 2), (2, 2), (4, 1), (5, 1))
+
+    def units(group):
+        return pl.ds(*GROUPS[group])
+
+    def weight_term(group):
+        unit, count = GROUPS[group]
+        if count == 2:
+            attended = jnp.concatenate([att_buf[0], att_buf[1]], axis=1)
+        else:
+            attended = att_buf[unit % 2]
         for t in range(8):
             both = dot(ogt[t * 192 : (t + 1) * 192, :], attended).astype(BF)
-            gbuf[2 * pair, t // 4, t % 4] = both[:, :HD]
-            gbuf[2 * pair + 1, t // 4, t % 4] = both[:, HD:]
-
-    def mate_copy(j):
-        return pltpu.make_async_remote_copy(
-            src_ref=gbuf.at[2 * j + 1 - core], dst_ref=rbuf.at[j],
-            send_sem=dd_s.at[j], recv_sem=dd_r.at[j], device_id=at(wa_=mate), device_id_type=MESH,
-        )
-
-    def x1_copy(j, which):
-        return pltpu.make_async_remote_copy(
-            src_ref=abuf.at[j, :, x_far if which else x_a], dst_ref=x1buf.at[j, which],
-            send_sem=x1_s.at[j, which], recv_sem=x1_r.at[j, which],
+            for n in range(count):
+                gbuf[unit + n, t // 4, t % 4] = both[:, n * HD : (n + 1) * HD]
+
+    def mate_copy(g):
+        return pltpu.make_async_remote_copy(
+            src_ref=gbuf.at[units(g), 1 - core], dst_ref=rbuf.at[units(g)],
+            send_sem=dd_s.at[0], recv_sem=dd_r.at[g], device_id=at(wa_=mate), device_id_type=MESH,
+        )
+
+    def x1_copy(g, which):
+        return pltpu.make_async_remote_copy(
+            src_ref=abuf.at[units(g), x_far if which else x_a], dst_ref=x1buf.at[which, units(g)],
+            send_sem=x1_s.at[0], recv_sem=x1_r.at[g, which],
             device_id=at(dp_=z_hi * 4 + x_a), device_id_type=MESH,
         )
 
-    def x2_copy(j):
-        return pltpu.make_async_remote_copy(
-            src_ref=xs.at[j], dst_ref=x2buf.at[j],
-            send_sem=x2_s.at[j], recv_sem=x2_r.at[j],
+    def x2_copy(g):
+        return pltpu.make_async_remote_copy(
+            src_ref=xs.at[units(g)], dst_ref=x2buf.at[units(g)],
+            send_sem=x2_s.at[0], recv_sem=x2_r.at[g],
             device_id=at(dp_=z_hi * 4 + x_b), device_id_type=MESH,
         )
 
-    def y_sum_copy(j, dy):
+    def y_sum_copy(g, dy):
         to = lax.rem(ha + dy, 4)
         return pltpu.make_async_remote_copy(
-            src_ref=cbuf.at[j, :, to], dst_ref=ybuf.at[dy - 1, j],
-            send_sem=yy_s.at[j, dy - 1], recv_sem=yy_r.at[j, dy - 1],
+            src_ref=cbuf.at[units(g), to], dst_ref=ybuf.at[dy - 1, units(g)],
+            send_sem=yy_s.at[0], recv_sem=yy_r.at[g],
             device_id=at(ha_=to), device_id_type=MESH,
         )
 
-    def z_sum_copy(dz):
-        return pltpu.make_async_remote_copy(
-            src_ref=zbuf.at[:, lax.rem(zi + dz, 8)], dst_ref=zr.at[dz - 1],
-            send_sem=zz_s.at[dz - 1], recv_sem=zz_r.at[dz - 1],
-            device_id=z_device(dz), device_id_type=MESH,
-        )
-
-    def last_copy():
-        return pltpu.make_async_remote_copy(
-            src_ref=fbuf.at[:, 1 - core], dst_ref=f2, send_sem=fin_s.at[0], recv_sem=fin_r.at[0],
-            device_id=at(wa_=mate), device_id_type=MESH,
+    Z_GROUPS = ((0, 2), (2, 1))
+
+    def z_sum_copy(n, shift, other):
+        target = lax.rem(z_lo + shift, 4) * 2 + (1 - core if other else core)
+        return pltpu.make_async_remote_copy(
+            src_ref=zbuf.at[target, pl.ds(*Z_GROUPS[n])],
+            dst_ref=zr.at[z_hi * 4 + shift, pl.ds(*Z_GROUPS[n])],
+            send_sem=zz_s.at[0], recv_sem=zz_r.at[n],
+            device_id=z_target(shift, other), device_id_type=MESH,
         )
 
     def wide(value):
         return value.astype(F32)
 
-    def add_mate(j):
-        mate_copy(j).wait_recv()
+    def unit_range(g):
+        return range(GROUPS[g][0], GROUPS[g][0] + GROUPS[g][1])
+
+    def add_mate(g):
+        mate_copy(g).wait_recv()
 
         def add(at_x):
-            for h in range(2):
-                abuf[j, h, at_x] = (
-                    wide(gbuf[2 * j + core, h, at_x]) + wide(rbuf[j, h, at_x])
-                ).astype(BF)
+            for u in unit_range(g):
+                abuf[u, at_x] = (wide(gbuf[u, core, at_x]) + wide(rbuf[u, at_x])).astype(BF)
 
         add(x_far)
-        x1_copy(j, 1).start()
+        x1_copy(g, 1).start()
         add(x_a)
-        x1_copy(j, 0).start()
+        x1_copy(g, 0).start()
         add(x_b)
         add(x)
 
-    def add_x1(j):
-        x1_copy(j, 1).wait_recv()
-        for h in range(2):
-            xs[j, h] = (wide(abuf[j, h, x_b]) + wide(x1buf[j, 1, h])).astype(BF)
-        x2_copy(j).start()
-
-    def add_x2(j):
-        x1_copy(j, 0).wait_recv()
-        x2_copy(j).wait_recv()
-        for h in range(2):
-            total = wide(abuf[j, h, x]) + wide(x1buf[j, 0, h]) + wide(x2buf[j, h])
-            cbuf[j, h] = total.astype(BF).reshape(4, 48, HD)
+    def add_x1(g):
+        x1_copy(g, 1).wait_recv()
+        for u in unit_range(g):
+            xs[u] = (wide(abuf[u, x_b]) + wide(x1buf[1, u])).astype(BF)
+        x2_copy(g).start()
+
+    def add_x2(g):
+        x1_copy(g, 0).wait_recv()
+        x2_copy(g).wait_recv()
+        for u in unit_range(g):
+            total = wide(abuf[u, x]) + wide(x1buf[0, u]) + wide(x2buf[u])
+            cbuf[u] = total.astype(BF).reshape(4, 48, HD)
         for dy in (2, 1, 3):
-            y_sum_copy(j, dy).start()
+            y_sum_copy(g, dy).start()
+
+    def wait_y(g):
+        pltpu.make_async_copy(ybuf.at[:, units(g)], ybuf.at[:, units(g)], yy_r.at[g]).wait()
 
     pick = (lax.broadcasted_iota(jnp.int32, (128, 96), 0), lax.broadcasted_iota(jnp.int32, (128, 96), 1))
-
     spread = (
-        ((pick[0] & 7) < 6) & (pick[1] == (pick[0] >> 3) * 6 + (pick[0] & 7))
+        ((pick[0] & 7) < 6)
+        & (pick[1] == ((pick[0] >> 3) & 1) * 48 + (pick[0] >> 4) * 6 + (pick[0] & 7))
     ).astype(F32).astype(BF)
 
-    def add_y(j):
-        for dy in (1, 2, 3):
-            y_sum_copy(j, dy).wait_recv()
+    def add_y(pair):
         halves = []
-        for h in range(2):
-            total = wide(cbuf[j, h, ha])
+        for u in (2 * pair, 2 * pair + 1):
+            total = wide(cbuf[u, ha])
             for n in range(3):
-                total = total + wide(ybuf[n, j, h])
+                total = total + wide(ybuf[n, u])
             halves.append(total.astype(BF))
         rows = dot(spread, jnp.concatenate(halves, axis=0))
-        zbuf[j] = rows.astype(BF).reshape(8, 16, HD)
-
-    def send_z():
-        for dz in (4, 3, 5, 2, 6, 1, 7):
-            z_sum_copy(dz).start()
+        zbuf[:, pair] = rows.astype(BF).reshape(8, 16, HD)
+
+    def send_z(n):
+        for shift in (2, 1, 3, 0):
+            z_sum_copy(n, shift, True).start()
+            if shift:
+                z_sum_copy(n, shift, False).start()
+
+        @pl.when(jnp.logical_not(own_z))
+        def _():
+            z_sum_copy(n, 0, False).start()
+
+        @pl.when(own_z)
+        def _():
+            pairs = range(Z_GROUPS[n][0], Z_GROUPS[n][0] + Z_GROUPS[n][1])
+            for pair in pairs:
+                zr[zi - z_lo, pair] = zbuf[z_lo * 2 + core, pair]
+
+    def z_bytes(ref, count, n):
+        part = ref.at[0:count, pl.ds(*Z_GROUPS[n])]
+        return part, part
 
     def add_z():
-        for dz in range(1, 8):
-            z_sum_copy(dz).wait_recv()
-        for j in range(3):
-            total = wide(zbuf[j, zi])
-            for n in range(7):
-                total = total + wide(zr[n, j])
-            fbuf[j] = total.reshape(2, 8, HD)
-        last_copy().start()
-
-    def finish_weights():
-        last_copy().wait_recv()
-        for j in range(3):
-            gws[2 * j + core] = fbuf[j, core]
-            gws[2 * j + 1 - core] = f2[j]
+        for n in range(2):
+            @pl.when(own_z)
+            def _(n=n):
+                pltpu.make_async_copy(*z_bytes(zr, 7, n), zz_r.at[n]).wait()
+
+            @pl.when(jnp.logical_not(own_z))
+            def _(n=n):
+                pltpu.make_async_copy(*z_bytes(zr, 8, n), zz_r.at[n]).wait()
+        for pair in range(3):
+            total = wide(zr[0, pair])
+            for n in range(1, 8):
+                total = total + wide(zr[n, pair])
+            gws[2 * pair] = total[:8]
+            gws[2 * pair + 1] = total[8:]
         for h in range(HEADS):
             gw_out[:, h * HD : (h + 1) * HD] = head_value(lambda s: gws[(s + 1) % HEADS, 0:6, :], h)
 
@@ -461,9 +488,9 @@
                 for op, *args in ops:
                     op(*args)
 
-    def pair_done(pair):
-        weight_term(pair)
-        mate_copy(pair).start()
+    def group_done(g):
+        weight_term(g)
+        mate_copy(g).start()
 
     forward(HALO, qa0[0], qa0[1], kv0[0], kv0[1], None)
     relay_kv(0)
@@ -487,10 +514,10 @@
         4: [(relay_qa, 1)],
     }
     AFTER_FORWARD = {
-        0: [(pair_done, 0)],
-        2: [(pair_done, 1)],
-        3: [(add_mate, 0)],
-        4: [(pair_done, 2)],
+        0: [(group_done, 0)],
+        2: [(group_done, 1), (add_mate, 0)],
+        3: [(group_done, 2)],
+        4: [(group_done, 3)],
     }
     lax.fori_loop(0, HALO, forward_step, 0)
 
@@ -498,14 +525,14 @@
 
     def sy_copy(r):
         return pltpu.make_async_remote_copy(
-            src_ref=sb.at[1, 1], dst_ref=sb.at[r, 1], send_sem=sy_s.at[r // 2], recv_sem=sy_r.at[r // 2],
+            src_ref=sb.at[1, 1], dst_ref=sb.at[r, 1], send_sem=sy_s.at[0], recv_sem=sy_r.at[r // 2],
             device_id=at(ha_=ha_up if r == 2 else ha_down), device_id_type=MESH,
         )
 
     def sw_copy(r, c):
         return pltpu.make_async_remote_copy(
             src_ref=sb.at[r, 1], dst_ref=sb.at[r, c],
-            send_sem=sw_s.at[r, c // 2], recv_sem=sw_r.at[r, c // 2],
+            send_sem=sw_s.at[c // 2], recv_sem=sw_r.at[c // 2],
             device_id=at(wa_=wa_right if c == 0 else wa_left), device_id_type=MESH,
         )
 
@@ -515,42 +542,46 @@
             def _(c=c):
                 sw_copy(r, c).start()
 
-    for r in (0, 2):
-        sy_copy(r).start()
-    sw_send(1)
-    relay_qa(2)
-    add_mate(1)
-    add_x1(0)
-
     chosen = (lax.broadcasted_iota(jnp.int32, (16, HD), 0), lax.broadcasted_iota(jnp.int32, (16, HD), 1))
     first = (chosen[0] & 7) * 3 + (chosen[0] >> 3) * 64
     take = ((chosen[1] >= first) & (chosen[1] < first + 3) & ((chosen[0] & 7) < 6)).astype(F32).astype(BF)
-
-    relay_qa(3)
-    own = dot_nt(take, sb[1, 1])
-    backward(
-        HALO, kv0[0], kv0[1], qa0[0], qa0[1], own[HALO : HALO + 1, :], own[8 + HALO : 9 + HALO, :]
-    )
-    add_mate(2)
 
     def relay_stats():
         for r in (0, 2):
             sy_copy(r).wait_recv()
             sw_send(r)
 
-    relay_stats()
-    relay_qa(4)
-    add_x1(1)
-    add_x2(0)
-
     def wait_stats():
         for c in ANY_COLS:
             @pl.when(gets_from[c])
             def _(c=c):
-                for r in range(3):
-                    sw_copy(r, c).wait_recv()
-
+                pltpu.make_async_copy(sb.at[:, 1], sb.at[:, c], sw_r.at[c // 2]).wait()
+
+    def backward_zero():
+        own = dot_nt(take, sb[1, 1])
+        backward(
+            HALO, kv0[0], kv0[1], qa0[0], qa0[1], own[HALO : HALO + 1, :], own[8 + HALO : 9 + HALO, :]
+        )
+
+    for r in (0, 2):
+        sy_copy(r).start()
+    sw_send(1)
+    add_mate(1)
+    add_mate(2)
+    relay_qa(2)
+    backward_zero()
+    add_mate(3)
+    relay_qa(3)
+    add_x1(0)
+    relay_stats()
+    relay_qa(4)
+    add_x1(1)
     add_x1(2)
+    add_x2(0)
+    add_x1(3)
+    add_x2(1)
+    add_x2(2)
+    add_x2(3)
     wait_stats()
     trow[...] = dot_nt(take, sb[...].reshape(KEYS, HD))
 
@@ -564,9 +595,8 @@
         return carry
 
     AFTER_BACKWARD = {
-        0: [(add_x2, 1), (add_x2, 2)],
-        1: [(add_y, 0)],
-        2: [(add_y, 1), (add_y, 2), (send_z,)],
+        0: [(wait_y, 0), (wait_y, 1), (add_y, 0), (add_y, 1), (send_z, 0)],
+        1: [(wait_y, 2), (wait_y, 3), (add_y, 2), (send_z, 1)],
     }
     lax.fori_loop(0, HALO, backward_step, 0)
 
@@ -576,41 +606,40 @@
             for n in range(3):
                 grads_out[n, :, cols] = head_value(lambda s: res[n, s], h)
 
-    place_outputs()
-    add_z()
-    finish_weights()
-
-    def sent(s, carry):
-        for r in (0, 2):
-            y_copy(kv, yk_s, yk_r, s, r).wait_send()
-            y_copy(qa, yq_s, yq_r, s, r).wait_send()
+    def left(ref, sem):
+        pltpu.make_async_copy(ref, ref, sem).wait()
+
+    def wait_sent():
+        for buf, y_send, w_sent in ((kv, yk_s, wk_s), (qa, yq_s, wq_s)):
+            for r in (0, 2):
+                left(buf.at[:, :, r, 1], y_send.at[r // 2])
+            for c in ANY_COLS:
+                @pl.when(sends_to[c])
+                def _(c=c, buf=buf, w_sent=w_sent):
+                    left(buf.at[:, :, :, c], w_sent.at[c // 2])
+        left(sb.at[0, 0:2], sy_s.at[0])
         for c in ANY_COLS:
             @pl.when(sends_to[c])
             def _(c=c):
-                for r in range(3):
-                    w_copy(kv, wk_s, wk_r, s, r, c).wait_send()
-                    w_copy(qa, wq_s, wq_r, s, r, c).wait_send()
-        return carry
-
-    lax.fori_loop(0, HALO, sent, 0)
-    for r in (0, 2):
-        sy_copy(r).wait_send()
-    for c in ANY_COLS:
-        @pl.when(sends_to[c])
-        def _(c=c):
-            for r in range(3):
-                sw_copy(r, c).wait_send()
-    for j in range(3):
-        mate_copy(j).wait_send()
-        x1_copy(j, 0).wait_send()
-        x1_copy(j, 1).wait_send()
-        x2_copy(j).wait_send()
-    for j in range(3):
-        for dy in (1, 2, 3):
-            y_sum_copy(j, dy).wait_send()
-    for dz in range(1, 8):
-        z_sum_copy(dz).wait_send()
-    last_copy().wait_send()
+                left(sb.at[:, c], sw_s.at[c // 2])
+        left(rbuf, dd_s.at[0])
+        left(x1buf, x1_s.at[0])
+        left(x2buf, x2_s.at[0])
+        left(ybuf, yy_s.at[0])
+
+    def flush():
+        @pl.when(own_z)
+        def _():
+            left(zr.at[0:7], zz_s.at[0])
+
+        @pl.when(jnp.logical_not(own_z))
+        def _():
+            left(zr, zz_s.at[0])
+
+    place_outputs()
+    wait_sent()
+    add_z()
+    flush()
 
 
 def put_out(grads, gw, gq_out, gk_out, gv_out, gw_out, sem):
@@ -636,15 +665,17 @@
         vm((TILE, HD), F32), vm((3, 3, TILE, HD), BF), vm((16, KEYS), F32),
         vm((TILE, KEYS), F32), vm((TILE, KEYS), F32), vm((TILE, KEYS), BF), vm((TILE, KEYS), BF),
         vm((2, TILE, HD), BF), vm((3, HEADS, TILE, HD), BF),
-        vm((6, 2, 4, 192, HD), BF), vm((3, 2, 4, 192, HD), BF), vm((3, 2, 4, 192, HD), BF),
-        vm((3, 2, 2, 192, HD), BF), vm((3, 2, 192, HD), BF), vm((3, 2, 192, HD), BF),
-        vm((3, 2, 4, 48, HD), BF), vm((3, 3, 2, 48, HD), BF),
-        vm((3, 8, 16, HD), BF), vm((7, 3, 16, HD), BF),
-        vm((3, 2, 8, HD), F32), vm((3, 8, HD), F32), vm((6, 8, HD), F32),
+        vm((6, 2, 4, 192, HD), BF), vm((6, 4, 192, HD), BF), vm((6, 4, 192, HD), BF),
+        vm((2, 6, 192, HD), BF), vm((6, 192, HD), BF), vm((6, 192, HD), BF),
+        vm((6, 4, 48, HD), BF), vm((3, 6, 48, HD), BF),
+        vm((8, 3, 16, HD), BF), vm((8, 3, 16, HD), BF), vm((6, 8, HD), F32),
         dma((6,)),
     ]
-    for extent in ((HALO, 2), (HALO, 2), (HALO, 3, 2), (HALO, 3, 2), (2,), (3, 2), (3,), (3, 2), (3,), (3, 3), (7,), (1,)):
-        shapes += [dma(extent), dma(extent)]
+    for sends, receives in (
+        ((2,), (HALO, 2)), ((2,), (HALO, 2)), ((2,), (HALO, 2)), ((2,), (HALO, 2)), ((1,), (2,)), ((2,), (2,)),
+        ((1,), (4,)), ((1,), (4, 2)), ((1,), (4,)), ((1,), (4,)), ((1,), (2,)),
+    ):
+        shapes += [dma(sends), dma(receives)]
     anywhere = pl.BlockSpec(memory_space=pl.ANY)
     inside = pl.BlockSpec(memory_space=pltpu.VMEM)
     grads, gw = pl.pallas_call(

time: 52.2 us -> 48.6 us (0.931)
  Pallas kernels: 51.4 us -> 47.9 us
    pallas_call x1, Pallas kernels: 50.6 us -> 47 us  [shards(): pl.pallas_call(kernel, out_shape=(pltpu.VMEM((3, TILE, HQ), BF), pltpu.VM...]
where the time goes in v3:
time: 48.6 us; the launch traced here: 48.5 us
  Pallas kernels  47.9 us (99%)
  between operations  0.64 us (1%)
    pallas_call x1, Pallas kernels, shards(): pl.pallas_call(kernel, out_shape=(pltpu.VMEM((3, TILE, HQ), BF), pltpu.VM...  47 us

profile of v3, /device:TPU:1, one launch (start us, length us, event | category | flops | bytes accessed | tf_op | source)
XLA Modules:
  0.0 48.5 jit_solution(8501858667501096333)
XLA Ops:
  0.6 47.0 %shard_map.93 = (bf16[3,144,768]{2,1,0:T(8,128)(2,1)S(1)}, f32[6,768]{1,0:T(8,128)S(1)}) custom-call(s32[6,6]{1,0:T(8,128)} %reach_in.1, bf16[144,768]{1,0:T(8,128)(2,1)} %bitcast.8, bf16[144,768]{1,0:T(8,128)(2,1)} %bitcast.9, bf16[144,768]{1,0:T(8,128)(2,1)} %bitcast.10, bf16[144,1536]{1,0:T(8,128)(2,1)} %bitcast.7, bf16[1536,768]{1,0:T(8,128)(2,1)} %w_in.1), custom_call_target="tpu_custom_call" | custom-call | tf_op jit(solution)/shard_map/pallas_call | solution.py:681
  47.6 0.9 %shard_map.94 = (bf16[144,768]{1,0:T(8,128)(2,1)}, bf16[144,768]{1,0:T(8,128)(2,1)}, bf16[144,768]{1,0:T(8,128)(2,1)}, f32[6,768]{1,0:T(8,128)}) custom-call(bf16[3,144,768]{2,1,0:T(8,128)(2,1)S(1)} %get-tuple-element.10.grads, f32[6,768]{1,0:T(8,128)S(1)} %get-tuple-element.11.gw), custom_call_target="tpu_custom_call" | custom-call | tf_op jit(solution)/shard_map/pallas_call | solution.py:697

commit v4 on v3

--- a/solution.py
+++ b/solution.py
@@ -21,6 +21,7 @@
 BF = jnp.bfloat16
 F32 = jnp.float32
 ANY_COLS = (0, 2)
+Z_FIRST = 2
 
 
 def dot(a, b):
@@ -38,7 +39,7 @@
     s_buf, dp_buf, p_buf, ds_buf, att_buf, res,
     gbuf, rbuf, abuf, x1buf, xs, x2buf, cbuf, ybuf, zbuf, zr, gws,
     in_sem, yk_s, yk_r, yq_s, yq_r, wk_s, wk_r, wq_s, wq_r, sy_s, sy_r, sw_s, sw_r,
-    dd_s, dd_r, x1_s, x1_r, x2_s, x2_r, yy_s, yy_r, zz_s, zz_r,
+    dd_s, dd_r, x1_s, x1_r, x2_s, x2_r, yy_s, yy_r, zz_s, zz_r, yc_s, yc_r,
 ):
     dp = lax.axis_index("dp")
     ha = lax.axis_index("ha")
@@ -203,8 +204,51 @@
     def relay_kv(s):
         relay(kv, yk_s, yk_r, wk_s, wk_r, s)
 
+    off_chip = {0: core == 0, 2: core == 1}
+    leaves_chip = {0: core == 1, 2: core == 0}
+
     def relay_qa(s):
-        relay(qa, yq_s, yq_r, wq_s, wq_r, s)
+        if s < Z_FIRST:
+            relay(qa, yq_s, yq_r, wq_s, wq_r, s)
+            return
+        for r in (0, 2):
+            y_copy(qa, yq_s, yq_r, s, r).wait_recv()
+            for c in ANY_COLS:
+                @pl.when(jnp.logical_not(leaves_chip[c]))
+                def _(c=c, r=r):
+                    w_copy(qa, wq_s, wq_r, s, r, c).start()
+
+    def corner_copy(s, r, c):
+        return pltpu.make_async_remote_copy(
+            src_ref=qa.at[s, :, 1, c], dst_ref=qa.at[s, :, r, c],
+            send_sem=yc_s.at[r // 2], recv_sem=yc_r.at[s - Z_FIRST, r // 2],
+            device_id=at(ha_=ha_up if r == 2 else ha_down), device_id_type=MESH,
+        )
+
+    def relay_corner(s):
+        for c in ANY_COLS:
+            @pl.when(gets_from[c] & off_chip[c])
+            def _(c=c):
+                w_copy(qa, wq_s, wq_r, s, 1, c).wait_recv()
+                for r in (0, 2):
+                    corner_copy(s, r, c).start()
+
+    def wait_qa(s):
+        @pl.when(s < Z_FIRST)
+        def _():
+            w_wait(qa, wq_s, wq_r, s)
+
+        @pl.when(s >= Z_FIRST)
+        def _():
+            for c in ANY_COLS:
+                @pl.when(jnp.logical_not(off_chip[c]))
+                def _(c=c):
+                    pltpu.make_async_copy(qa.at[s, :, :, 1], qa.at[s, :, :, c], wq_r.at[s, c // 2]).wait()
+
+                @pl.when(gets_from[c] & off_chip[c])
+                def _(c=c):
+                    for r in (0, 2):
+                        corner_copy(s, r, c).wait_recv()
 
     def wait_barrier():
         pl.semaphore_wait(barrier, 14 - 2 * own_z.astype(jnp.int32) + (far_right | far_left).astype(jnp.int32))
@@ -327,7 +371,7 @@
         res[2, slot] = dot(p_buf[:, :n], a).astype(BF)
         res[1, slot] = (dot(ds_buf[:, :n], q) * SCALE).astype(BF)
 
-    GROUPS = ((0, 2), (2, 2), (4, 1), (5, 1))
+    GROUPS = tuple((unit, 1) for unit in range(HEADS))
 
     def units(group):
         return pl.ds(*GROUPS[group])
@@ -475,11 +519,8 @@
             gw_out[:, h * HD : (h + 1) * HD] = head_value(lambda s: gws[(s + 1) % HEADS, 0:6, :], h)
 
     def own_qa():
-        def step(t, c):
-            w_send(qa, wq_s, wq_r, t, 1)
-            return c
-
-        lax.fori_loop(0, HALO, step, 0)
+        for s in (2, 3, 4, 0, 1):
+            w_send(qa, wq_s, wq_r, s, 1)
 
     def hooked(s, hooks):
         for n, ops in hooks.items():
@@ -493,6 +534,7 @@
         mate_copy(g).start()
 
     forward(HALO, qa0[0], qa0[1], kv0[0], kv0[1], None)
+    group_done(0)
     relay_kv(0)
     relay_kv(1)
 
@@ -514,10 +556,11 @@
         4: [(relay_qa, 1)],
     }
     AFTER_FORWARD = {
-        0: [(group_done, 0)],
-        2: [(group_done, 1), (add_mate, 0)],
-        3: [(group_done, 2)],
-        4: [(group_done, 3)],
+        0: [(group_done, 1), (add_mate, 0)],
+        1: [(group_done, 2), (add_mate, 1)],
+        2: [(group_done, 3), (add_mate, 2), (add_x1, 0)],
+        3: [(group_done, 4), (add_mate, 3), (add_x1, 1)],
+        4: [(group_done, 5), (add_mate, 4), (add_x1, 2), (add_x2, 0)],
     }
     lax.fori_loop(0, HALO, forward_step, 0)
 
@@ -566,27 +609,26 @@
     for r in (0, 2):
         sy_copy(r).start()
     sw_send(1)
-    add_mate(1)
-    add_mate(2)
+    relay_corner(2)
+    relay_corner(3)
+    relay_corner(4)
     relay_qa(2)
     backward_zero()
-    add_mate(3)
+    add_mate(5)
+    add_x1(3)
     relay_qa(3)
-    add_x1(0)
+    add_x2(1)
     relay_stats()
+    add_x1(4)
     relay_qa(4)
-    add_x1(1)
-    add_x1(2)
-    add_x2(0)
-    add_x1(3)
-    add_x2(1)
     add_x2(2)
+    add_x1(5)
     add_x2(3)
     wait_stats()
     trow[...] = dot_nt(take, sb[...].reshape(KEYS, HD))
 
     def backward_step(s, carry):
-        w_wait(qa, wq_s, wq_r, s)
+        wait_qa(s)
         backward(
             s, kv[s, 0, 1, 1], kv[s, 1, 1, 1], qa[s, 0].reshape(KEYS, HD), qa[s, 1].reshape(KEYS, HD),
             trow[pl.ds(s, 1), :] - bias_row(s, True), trow[pl.ds(s + 8, 1), :],
@@ -595,8 +637,11 @@
         return carry
 
     AFTER_BACKWARD = {
-        0: [(wait_y, 0), (wait_y, 1), (add_y, 0), (add_y, 1), (send_z, 0)],
-        1: [(wait_y, 2), (wait_y, 3), (add_y, 2), (send_z, 1)],
+        0: [
+            (add_x2, 4), (add_x2, 5), (wait_y, 0), (wait_y, 1), (wait_y, 2), (wait_y, 3),
+            (add_y, 0), (add_y, 1), (send_z, 0),
+        ],
+        2: [(wait_y, 4), (wait_y, 5), (add_y, 2), (send_z, 1)],
     }
     lax.fori_loop(0, HALO, backward_step, 0)
 
@@ -614,9 +659,24 @@
             for r in (0, 2):
                 left(buf.at[:, :, r, 1], y_send.at[r // 2])
             for c in ANY_COLS:
-                @pl.when(sends_to[c])
-                def _(c=c, buf=buf, w_sent=w_sent):
-                    left(buf.at[:, :, :, c], w_sent.at[c // 2])
+                if buf is kv:
+                    @pl.when(sends_to[c])
+                    def _(c=c):
+                        left(kv.at[:, :, :, c], wk_s.at[c // 2])
+                    continue
+
+                @pl.when(jnp.logical_not(leaves_chip[c]))
+                def _(c=c):
+                    left(qa.at[:, :, :, c], wq_s.at[c // 2])
+
+                @pl.when(sends_to[c] & leaves_chip[c])
+                def _(c=c):
+                    left(qa.at[0], wq_s.at[c // 2])
+        for c in ANY_COLS:
+            @pl.when(gets_from[c] & off_chip[c])
+            def _(c=c):
+                for r in (0, 2):
+                    left(qa.at[0, 0, 0:2], yc_s.at[r // 2])
         left(sb.at[0, 0:2], sy_s.at[0])
         for c in ANY_COLS:
             @pl.when(sends_to[c])
@@ -673,7 +733,7 @@
     ]
     for sends, receives in (
         ((2,), (HALO, 2)), ((2,), (HALO, 2)), ((2,), (HALO, 2)), ((2,), (HALO, 2)), ((1,), (2,)), ((2,), (2,)),
-        ((1,), (4,)), ((1,), (4, 2)), ((1,), (4,)), ((1,), (4,)), ((1,), (2,)),
+        ((1,), (6,)), ((1,), (6, 2)), ((1,), (6,)), ((1,), (6,)), ((1,), (2,)), ((2,), (HALO - Z_FIRST, 2)),
     ):
         shapes += [dma(sends), dma(receives)]
     anywhere = pl.BlockSpec(memory_space=pl.ANY)

time: 48.6 us -> 45.8 us (0.942)
  Pallas kernels: 47.9 us -> 45 us
    pallas_call x1, Pallas kernels: 47 us -> 44.1 us  [shards(): pl.pallas_call(kernel, out_shape=(pltpu.VMEM((3, TILE, HQ), BF), pltpu.VM...]
where the time goes in v4:
time: 45.8 us; the launch traced here: 45.6 us
  Pallas kernels  45 us (98%)
  between operations  0.64 us (1%)
    pallas_call x1, Pallas kernels, shards(): pl.pallas_call(kernel, out_shape=(pltpu.VMEM((3, TILE, HQ), BF), pltpu.VM...  44.1 us

profile of v4, /device:TPU:1, one launch (start us, length us, event | category | flops | bytes accessed | tf_op | source)
XLA Modules:
  0.0 45.6 jit_solution(3854425515471566329)
XLA Ops:
  0.6 44.1 %shard_map.93 = (bf16[3,144,768]{2,1,0:T(8,128)(2,1)S(1)}, f32[6,768]{1,0:T(8,128)S(1)}) custom-call(s32[6,6]{1,0:T(8,128)} %reach_in.1, bf16[144,768]{1,0:T(8,128)(2,1)} %bitcast.8, bf16[144,768]{1,0:T(8,128)(2,1)} %bitcast.9, bf16[144,768]{1,0:T(8,128)(2,1)} %bitcast.10, bf16[144,1536]{1,0:T(8,128)(2,1)} %bitcast.7, bf16[1536,768]{1,0:T(8,128)(2,1)} %w_in.1), custom_call_target="tpu_custom_call" | custom-call | tf_op jit(solution)/shard_map/pallas_call | solution.py:741
  44.8 0.9 %shard_map.94 = (bf16[144,768]{1,0:T(8,128)(2,1)}, bf16[144,768]{1,0:T(8,128)(2,1)}, bf16[144,768]{1,0:T(8,128)(2,1)}, f32[6,768]{1,0:T(8,128)}) custom-call(bf16[3,144,768]{2,1,0:T(8,128)(2,1)S(1)} %get-tuple-element.10.grads, f32[6,768]{1,0:T(8,128)S(1)} %get-tuple-element.11.gw), custom_call_target="tpu_custom_call" | custom-call | tf_op jit(solution)/shard_map/pallas_call | solution.py:757

commit v5 on v4

--- a/solution.py
+++ b/solution.py
@@ -16,12 +16,15 @@
 HQ = HEADS * HD
 D = 1536
 SCALE = 1.0 / math.sqrt(HD)
+LOG2E = 1.0 / math.log(2.0)
+SCALE2 = SCALE * LOG2E
 ROWS = 16
 FORWARD_UNROLL = 9
 BF = jnp.bfloat16
 F32 = jnp.float32
 ANY_COLS = (0, 2)
-Z_FIRST = 2
+DIRECT = 4
+Z_FIRST = 3
 
 
 def dot(a, b):
@@ -37,9 +40,9 @@
     grads_out, gw_out,
     reach, q_v, k_v, v_v, og_v, w_v, a_v, ogt, kv, qa, kv0, qa0, stat, sb, trow,
     s_buf, dp_buf, p_buf, ds_buf, att_buf, res,
-    gbuf, rbuf, abuf, x1buf, xs, x2buf, cbuf, ybuf, zbuf, zr, gws,
+    gbuf, rbuf, abuf, x1buf, xs, x2buf, cbuf, ybuf, xbuf, yxbuf, zbuf, zr, gws,
     in_sem, yk_s, yk_r, yq_s, yq_r, wk_s, wk_r, wq_s, wq_r, sy_s, sy_r, sw_s, sw_r,
-    dd_s, dd_r, x1_s, x1_r, x2_s, x2_r, yy_s, yy_r, zz_s, zz_r, yc_s, yc_r,
+    dd_s, dd_r, x1_s, x1_r, x2_s, x2_r, yy_s, yy_r, zz_s, zz_r, yc_s, yc_r, yx_s, yx_r, zq_s,
 ):
     dp = lax.axis_index("dp")
     ha = lax.axis_index("ha")
@@ -77,6 +80,7 @@
 
     for dy in (1, 2, 3):
         greet(at(ha_=lax.rem(ha + dy, 4)))
+        greet(at(dp_=z_hi * 4 + x_b, ha_=lax.rem(ha + dy, 4)))
     greet(at(wa_=mate))
     greet(at(dp_=z_hi * 4 + x_one))
     greet(at(dp_=z_hi * 4 + x_three))
@@ -225,6 +229,13 @@
             device_id=at(ha_=ha_up if r == 2 else ha_down), device_id_type=MESH,
         )
 
+    def z_first_copy(s, c):
+        return pltpu.make_async_remote_copy(
+            src_ref=qa.at[s, :, 1, 1], dst_ref=qa.at[s, :, 1, c],
+            send_sem=zq_s.at[0], recv_sem=wq_r.at[s, c // 2],
+            device_id=at(wa_=wa_right if c == 0 else wa_left), device_id_type=MESH,
+        )
+
     def relay_corner(s):
         for c in ANY_COLS:
             @pl.when(gets_from[c] & off_chip[c])
@@ -251,7 +262,7 @@
                         corner_copy(s, r, c).wait_recv()
 
     def wait_barrier():
-        pl.semaphore_wait(barrier, 14 - 2 * own_z.astype(jnp.int32) + (far_right | far_left).astype(jnp.int32))
+        pl.semaphore_wait(barrier, 17 - 2 * own_z.astype(jnp.int32) + (far_right | far_left).astype(jnp.int32))
 
     wait_barrier()
 
@@ -333,19 +344,19 @@
 
         def rows_step(i, carry):
             rows = pl.ds(pl.multiple_of(i * ROWS, ROWS), ROWS)
-            s = s_buf[rows, :n] * SCALE
+            s = s_buf[rows, :n] * SCALE2
             if bias is not None:
                 s = s + bias
             d = dp_buf[rows, :n]
             peak = jnp.max(s, axis=1, keepdims=True)
-            e = jnp.exp(s - peak)
+            e = jnp.exp2(s - peak)
             total = jnp.sum(e, axis=1, keepdims=True)
             p = e * (1.0 / total)
             delta = jnp.sum(p * d, axis=1, keepdims=True)
             p_buf[rows, :n] = p.astype(BF)
             ds_buf[rows, :n] = (p * (d - delta)).astype(BF)
             block = stat[rows, :]
-            for base, parts in ((0, split3(peak + jnp.log(total))), (64, split3(delta))):
+            for base, parts in ((0, split3(peak + jnp.log(total) * LOG2E)), (64, split3(delta))):
                 for t, part in enumerate(parts):
                     block = jnp.where(lane == base + 3 * slot + t, part, block)
             stat[rows, :] = block
@@ -362,7 +373,7 @@
 
         def rows_step(i, carry):
             rows = pl.ds(pl.multiple_of(i * ROWS, ROWS), ROWS)
-            p = jnp.exp(s_buf[rows, :n] * SCALE - lse_row)
+            p = jnp.exp2(s_buf[rows, :n] * SCALE2 - lse_row)
             p_buf[rows, :n] = p.astype(BF)
             ds_buf[rows, :n] = (p * (dp_buf[rows, :n] - delta_row)).astype(BF)
             return carry
@@ -415,6 +426,14 @@
             device_id=at(ha_=to), device_id_type=MESH,
         )
 
+    def across_copy(u, dy):
+        to = lax.rem(ha + dy, 4)
+        return pltpu.make_async_remote_copy(
+            src_ref=xbuf.at[u - DIRECT, to], dst_ref=yxbuf.at[dy, u - DIRECT],
+            send_sem=yx_s.at[0], recv_sem=yx_r.at[u - DIRECT],
+            device_id=at(dp_=z_hi * 4 + x_b, ha_=to), device_id_type=MESH,
+        )
+
     Z_GROUPS = ((0, 2), (2, 1))
 
     def z_sum_copy(n, shift, other):
@@ -464,6 +483,22 @@
     def wait_y(g):
         pltpu.make_async_copy(ybuf.at[:, units(g)], ybuf.at[:, units(g)], yy_r.at[g]).wait()
 
+    def add_direct(u):
+        x1_copy(u, 1).wait_recv()
+        total = wide(abuf[u, x_b]) + wide(x1buf[1, u])
+        xbuf[u - DIRECT] = total.astype(BF).reshape(4, 48, HD)
+        for dy in (2, 1, 3, 0):
+            across_copy(u, dy).start()
+        x1_copy(u, 0).wait_recv()
+        total = wide(abuf[u, x]) + wide(x1buf[0, u])
+        cbuf[u] = total.astype(BF).reshape(4, 48, HD)
+        for dy in (2, 1, 3):
+            y_sum_copy(u, dy).start()
+
+    def wait_direct(u):
+        wait_y(u)
+        pltpu.make_async_copy(yxbuf.at[:, u - DIRECT], yxbuf.at[:, u - DIRECT], yx_r.at[u - DIRECT]).wait()
+
     pick = (lax.broadcasted_iota(jnp.int32, (128, 96), 0), lax.broadcasted_iota(jnp.int32, (128, 96), 1))
     spread = (
         ((pick[0] & 7) < 6)
@@ -476,6 +511,9 @@
             total = wide(cbuf[u, ha])
             for n in range(3):
                 total = total + wide(ybuf[n, u])
+            if u >= DIRECT:
+                for n in range(4):
+                    total = total + wide(yxbuf[n, u - DIRECT])
             halves.append(total.astype(BF))
         rows = dot(spread, jnp.concatenate(halves, axis=0))
         zbuf[:, pair] = rows.astype(BF).reshape(8, 16, HD)
@@ -519,7 +557,16 @@
             gw_out[:, h * HD : (h + 1) * HD] = head_value(lambda s: gws[(s + 1) % HEADS, 0:6, :], h)
 
     def own_qa():
-        for s in (2, 3, 4, 0, 1):
+        for s in range(Z_FIRST, HALO):
+            for c in ANY_COLS:
+                @pl.when(sends_to[c] & leaves_chip[c])
+                def _(c=c, s=s):
+                    z_first_copy(s, c).start()
+
+                @pl.when(jnp.logical_not(leaves_chip[c]))
+                def _(c=c, s=s):
+                    w_copy(qa, wq_s, wq_r, s, 1, c).start()
+        for s in range(Z_FIRST):
             w_send(qa, wq_s, wq_r, s, 1)
 
     def hooked(s, hooks):
@@ -534,7 +581,18 @@
         mate_copy(g).start()
 
     forward(HALO, qa0[0], qa0[1], kv0[0], kv0[1], None)
+    chosen = (lax.broadcasted_iota(jnp.int32, (16, HD), 0), lax.broadcasted_iota(jnp.int32, (16, HD), 1))
+    first = (chosen[0] & 7) * 3 + (chosen[0] >> 3) * 64
+    take = ((chosen[1] >= first) & (chosen[1] < first + 3) & ((chosen[0] & 7) < 6)).astype(F32).astype(BF)
+
+    def backward_zero():
+        own = dot_nt(take, stat[...].astype(BF))
+        backward(
+            HALO, kv0[0], kv0[1], qa0[0], qa0[1], own[HALO : HALO + 1, :], own[8 + HALO : 9 + HALO, :]
+        )
+
     group_done(0)
+    backward_zero()
     relay_kv(0)
     relay_kv(1)
 
@@ -550,17 +608,16 @@
 
     BEFORE_FORWARD = {
         0: [(relay_kv, 2)],
-        1: [(relay_kv, 3)],
-        2: [(relay_kv, 4), (own_qa,)],
+        2: [(own_qa,)],
         3: [(relay_qa, 0)],
         4: [(relay_qa, 1)],
     }
     AFTER_FORWARD = {
-        0: [(group_done, 1), (add_mate, 0)],
-        1: [(group_done, 2), (add_mate, 1)],
+        0: [(relay_kv, 3), (group_done, 1), (add_mate, 0)],
+        1: [(relay_kv, 4), (group_done, 2), (add_mate, 1)],
         2: [(group_done, 3), (add_mate, 2), (add_x1, 0)],
         3: [(group_done, 4), (add_mate, 3), (add_x1, 1)],
-        4: [(group_done, 5), (add_mate, 4), (add_x1, 2), (add_x2, 0)],
+        4: [(group_done, 5), (add_mate, 4), (add_x1, 2)],
     }
     lax.fori_loop(0, HALO, forward_step, 0)
 
@@ -585,10 +642,6 @@
             def _(c=c):
                 sw_copy(r, c).start()
 
-    chosen = (lax.broadcasted_iota(jnp.int32, (16, HD), 0), lax.broadcasted_iota(jnp.int32, (16, HD), 1))
-    first = (chosen[0] & 7) * 3 + (chosen[0] >> 3) * 64
-    take = ((chosen[1] >= first) & (chosen[1] < first + 3) & ((chosen[0] & 7) < 6)).astype(F32).astype(BF)
-
     def relay_stats():
         for r in (0, 2):
             sy_copy(r).wait_recv()
@@ -600,30 +653,23 @@
             def _(c=c):
                 pltpu.make_async_copy(sb.at[:, 1], sb.at[:, c], sw_r.at[c // 2]).wait()
 
-    def backward_zero():
-        own = dot_nt(take, sb[1, 1])
-        backward(
-            HALO, kv0[0], kv0[1], qa0[0], qa0[1], own[HALO : HALO + 1, :], own[8 + HALO : 9 + HALO, :]
-        )
-
     for r in (0, 2):
         sy_copy(r).start()
     sw_send(1)
-    relay_corner(2)
     relay_corner(3)
     relay_corner(4)
     relay_qa(2)
-    backward_zero()
     add_mate(5)
     add_x1(3)
+    add_x2(0)
     relay_qa(3)
     add_x2(1)
     relay_stats()
-    add_x1(4)
+    add_direct(4)
     relay_qa(4)
     add_x2(2)
-    add_x1(5)
     add_x2(3)
+    add_direct(5)
     wait_stats()
     trow[...] = dot_nt(take, sb[...].reshape(KEYS, HD))
 
@@ -638,10 +684,9 @@
 
     AFTER_BACKWARD = {
         0: [
-            (add_x2, 4), (add_x2, 5), (wait_y, 0), (wait_y, 1), (wait_y, 2), (wait_y, 3),
-            (add_y, 0), (add_y, 1), (send_z, 0),
+            (wait_y, 0), (wait_y, 1), (wait_y, 2), (wait_y, 3), (add_y, 0), (add_y, 1), (send_z, 0),
+            (wait_direct, 4), (wait_direct, 5), (add_y, 2), (send_z, 1),
         ],
-        2: [(wait_y, 4), (wait_y, 5), (add_y, 2), (send_z, 1)],
     }
     lax.fori_loop(0, HALO, backward_step, 0)
 
@@ -671,12 +716,13 @@
 
                 @pl.when(sends_to[c] & leaves_chip[c])
                 def _(c=c):
-                    left(qa.at[0], wq_s.at[c // 2])
+                    left(qa.at[0:Z_FIRST, :, :, c], wq_s.at[c // 2])
+                    left(qa.at[Z_FIRST:HALO, :, 1, c], zq_s.at[0])
         for c in ANY_COLS:
             @pl.when(gets_from[c] & off_chip[c])
             def _(c=c):
                 for r in (0, 2):
-                    left(qa.at[0, 0, 0:2], yc_s.at[r // 2])
+                    left(qa.at[Z_FIRST:HALO, :, r, c], yc_s.at[r // 2])
         left(sb.at[0, 0:2], sy_s.at[0])
         for c in ANY_COLS:
             @pl.when(sends_to[c])
@@ -686,6 +732,7 @@
         left(x1buf, x1_s.at[0])
         left(x2buf, x2_s.at[0])
         left(ybuf, yy_s.at[0])
+        left(yxbuf, yx_s.at[0])
 
     def flush():
         @pl.when(own_z)
@@ -726,16 +773,18 @@
         vm((TILE, KEYS), F32), vm((TILE, KEYS), F32), vm((TILE, KEYS), BF), vm((TILE, KEYS), BF),
         vm((2, TILE, HD), BF), vm((3, HEADS, TILE, HD), BF),
         vm((6, 2, 4, 192, HD), BF), vm((6, 4, 192, HD), BF), vm((6, 4, 192, HD), BF),
-        vm((2, 6, 192, HD), BF), vm((6, 192, HD), BF), vm((6, 192, HD), BF),
+        vm((2, 6, 192, HD), BF), vm((DIRECT, 192, HD), BF), vm((DIRECT, 192, HD), BF),
         vm((6, 4, 48, HD), BF), vm((3, 6, 48, HD), BF),
+        vm((HEADS - DIRECT, 4, 48, HD), BF), vm((4, HEADS - DIRECT, 48, HD), BF),
         vm((8, 3, 16, HD), BF), vm((8, 3, 16, HD), BF), vm((6, 8, HD), F32),
         dma((6,)),
     ]
     for sends, receives in (
         ((2,), (HALO, 2)), ((2,), (HALO, 2)), ((2,), (HALO, 2)), ((2,), (HALO, 2)), ((1,), (2,)), ((2,), (2,)),
-        ((1,), (6,)), ((1,), (6, 2)), ((1,), (6,)), ((1,), (6,)), ((1,), (2,)), ((2,), (HALO - Z_FIRST, 2)),
+        ((1,), (6,)), ((1,), (6, 2)), ((1,), (DIRECT,)), ((1,), (6,)), ((1,), (2,)), ((2,), (HALO - Z_FIRST, 2)), ((1,), (HEADS - DIRECT,)),
     ):
         shapes += [dma(sends), dma(receives)]
+    shapes.append(dma((1,)))
     anywhere = pl.BlockSpec(memory_space=pl.ANY)
     inside = pl.BlockSpec(memory_space=pltpu.VMEM)
     grads, gw = pl.pallas_call(

time: 45.8 us -> 45.2 us (0.987)
  Pallas kernels: 45 us -> 44.5 us
    pallas_call x1, Pallas kernels: 44.1 us -> 43.6 us  [shards(): pl.pallas_call(kernel, out_shape=(pltpu.VMEM((3, TILE, HQ), BF), pltpu.VM...]
where the time goes in v5:
time: 45.2 us; the launch traced here: 45.1 us
  Pallas kernels  44.5 us (98%)
  between operations  0.64 us (1%)
    pallas_call x1, Pallas kernels, shards(): pl.pallas_call(kernel, out_shape=(pltpu.VMEM((3, TILE, HQ), BF), pltpu.VM...  43.6 us

profile of v5, /device:TPU:1, one launch (start us, length us, event | category | flops | bytes accessed | tf_op | source)
XLA Modules:
  0.0 45.1 jit_solution(18043276825501849606)
XLA Ops:
  0.6 43.6 %shard_map.93 = (bf16[3,144,768]{2,1,0:T(8,128)(2,1)S(1)}, f32[6,768]{1,0:T(8,128)S(1)}) custom-call(s32[6,6]{1,0:T(8,128)} %reach_in.1, bf16[144,768]{1,0:T(8,128)(2,1)} %bitcast.8, bf16[144,768]{1,0:T(8,128)(2,1)} %bitcast.9, bf16[144,768]{1,0:T(8,128)(2,1)} %bitcast.10, bf16[144,1536]{1,0:T(8,128)(2,1)} %bitcast.7, bf16[1536,768]{1,0:T(8,128)(2,1)} %w_in.1), custom_call_target="tpu_custom_call" | custom-call | tf_op jit(solution)/shard_map/pallas_call | solution.py:790
  44.2 0.9 %shard_map.94 = (bf16[144,768]{1,0:T(8,128)(2,1)}, bf16[144,768]{1,0:T(8,128)(2,1)}, bf16[144,768]{1,0:T(8,128)(2,1)}, f32[6,768]{1,0:T(8,128)}) custom-call(bf16[3,144,768]{2,1,0:T(8,128)(2,1)S(1)} %get-tuple-element.10.grads, f32[6,768]{1,0:T(8,128)S(1)} %get-tuple-element.11.gw), custom_call_target="tpu_custom_call" | custom-call | tf_op jit(solution)/shard_map/pallas_call | solution.py:806

commit v6 on v5

--- a/solution.py
+++ b/solution.py
@@ -23,7 +23,7 @@
 BF = jnp.bfloat16
 F32 = jnp.float32
 ANY_COLS = (0, 2)
-DIRECT = 4
+DIRECT = 5
 Z_FIRST = 3
 
 
@@ -665,11 +665,12 @@
     relay_qa(3)
     add_x2(1)
     relay_stats()
-    add_direct(4)
+    add_x1(4)
     relay_qa(4)
     add_x2(2)
+    add_direct(5)
     add_x2(3)
-    add_direct(5)
+    add_x2(4)
     wait_stats()
     trow[...] = dot_nt(take, sb[...].reshape(KEYS, HD))
 
@@ -685,7 +686,7 @@
     AFTER_BACKWARD = {
         0: [
             (wait_y, 0), (wait_y, 1), (wait_y, 2), (wait_y, 3), (add_y, 0), (add_y, 1), (send_z, 0),
-            (wait_direct, 4), (wait_direct, 5), (add_y, 2), (send_z, 1),
+            (wait_y, 4), (wait_direct, 5), (add_y, 2), (send_z, 1),
         ],
     }
     lax.fori_loop(0, HALO, backward_step, 0)

time: 45.2 us -> 45.1 us (level)
  no operation moved by 1% of the time
where the time goes in v6:
time: 45.1 us; the launch traced here: 45 us
  Pallas kernels  44.4 us (98%)
  between operations  0.64 us (1%)
    pallas_call x1, Pallas kernels, shards(): pl.pallas_call(kernel, out_shape=(pltpu.VMEM((3, TILE, HQ), BF), pltpu.VM...  43.5 us

profile of v6, /device:TPU:1, one launch (start us, length us, event | category | flops | bytes accessed | tf_op | source)
XLA Modules:
  0.0 45.0 jit_solution(12649101426948603064)
XLA Ops:
  0.6 43.5 %shard_map.93 = (bf16[3,144,768]{2,1,0:T(8,128)(2,1)S(1)}, f32[6,768]{1,0:T(8,128)S(1)}) custom-call(s32[6,6]{1,0:T(8,128)} %reach_in.1, bf16[144,768]{1,0:T(8,128)(2,1)} %bitcast.8, bf16[144,768]{1,0:T(8,128)(2,1)} %bitcast.9, bf16[144,768]{1,0:T(8,128)(2,1)} %bitcast.10, bf16[144,1536]{1,0:T(8,128)(2,1)} %bitcast.7, bf16[1536,768]{1,0:T(8,128)(2,1)} %w_in.1), custom_call_target="tpu_custom_call" | custom-call | tf_op jit(solution)/shard_map/pallas_call | solution.py:791
  44.1 0.9 %shard_map.94 = (bf16[144,768]{1,0:T(8,128)(2,1)}, bf16[144,768]{1,0:T(8,128)(2,1)}, bf16[144,768]{1,0:T(8,128)(2,1)}, f32[6,768]{1,0:T(8,128)}) custom-call(bf16[3,144,768]{2,1,0:T(8,128)(2,1)S(1)} %get-tuple-element.10.grads, f32[6,768]{1,0:T(8,128)S(1)} %get-tuple-element.11.gw), custom_call_target="tpu_custom_call" | custom-call | tf_op jit(solution)/shard_map/pallas_call | solution.py:807
